TPU v7x, 32 devices: a whole 2x2x4 slice. The times are simulated.
32 devices in a mesh: band: 8 (over z, y), dom: 4 (over x, core).
Axes of the slice: x: 2, y: 2, z: 4, core: 2. Of those that a mesh axis runs over, the one named last changes fastest.
Arguments:
- wavefunctions: float32 [1024, 16, 16, 128], P('band', 'dom'), may hold values from -6 to 6
- potential: float32 [16, 16, 128], P('dom'), may hold values from -40 to 40
- projectors: float32 [16, 18, 4, 16, 128], P('dom'), may hold values from -0.0625 to 0.0625
- hamiltonian_correction: float32 [16, 18, 18], P('dom'), may hold values from -0.078125 to 0.078125
- delta_s: float32 [16, 18, 18], P('dom'), may hold values from -0.078125 to 0.078125
- projector_count: int32 [16], P('dom'), may hold values from 1 to 18
Outputs:
- ham: float32 [1024, 1024], P('band')
- correlation: float32 [1024, 1024], P('band')
All inputs are finite; a program needn't handle non-finite values.
Results may differ from a plain program's by a relative error of at most 0.00007.
Values sent between devices are 32-bit elements; how exact they have to be, the bound alone decides.
A program may use at most 192 MiB of HBM per device.

v0:
```python
import functools

import jax
import jax.numpy as jnp
from jax import lax
from jax.experimental import pallas as pl
from jax.experimental.pallas import tpu as pltpu
from jax.sharding import PartitionSpec as P

MESH = pl.DeviceIdType.MESH
CONTRACT_LAST = (((1,), (1,)), ((), ()))


def parts(value):
    high = value.astype(jnp.bfloat16)
    low = (value - high.astype(jnp.float32)).astype(jnp.bfloat16)
    return high, low


def gram_kernel(
    lines, doms, cx, ny, chunks,
    psi, pot, proj, sym, out,
    partner, halo, partner_halo, from_left, from_right, lhs_high, lhs_low,
    left_edges, right_edges, coef, coef_below,
    swap_send, swap_recv, halo_send, halo_recv, fwd_send, fwd_recv,
    right_send, right_recv, left_send, left_recv,
    right_edge_send, right_edge_recv, left_edge_send, left_edge_recv,
    coef_send, coef_recv, pair_send, pair_recv,
):
    rows, bands, nz = psi.shape
    half = rows // 2
    step = half // chunks
    hy = ny // 2
    mine = lax.axis_index("band")
    dom = lax.axis_index("dom")
    line = mine // 2
    side = mine % 2
    mirror = lines - 1 - line
    pair = line * 2 + (1 - side)
    upper = jnp.minimum(line + 1, lines - 1) * 2 + side
    lower = jnp.maximum(line - 1, 0) * 2 + side
    dom_next = (dom + 1) % doms
    dom_prev = (dom + doms - 1) % doms
    ends = lines >= 4

    barrier = pltpu.get_barrier_semaphore()
    pl.semaphore_signal(barrier, inc=1, device_id={"band": pair}, device_id_type=MESH)
    pl.semaphore_signal(barrier, inc=1, device_id={"dom": dom_next}, device_id_type=MESH)
    pl.semaphore_signal(barrier, inc=1, device_id={"dom": dom_prev}, device_id_type=MESH)

    @pl.when(line > 0)
    def _():
        pl.semaphore_signal(barrier, inc=1, device_id={"band": lower}, device_id_type=MESH)

    @pl.when(line < lines - 1)
    def _():
        pl.semaphore_signal(barrier, inc=1, device_id={"band": upper}, device_id_type=MESH)

    peers = 3 + jnp.minimum(line, 1) + jnp.minimum(mirror, 1)
    pl.semaphore_wait(barrier, peers)

    def remote(src, dst, send, recv, where):
        return pltpu.make_async_remote_copy(
            src_ref=src, dst_ref=dst, send_sem=send, recv_sem=recv,
            device_id=where, device_id_type=MESH,
        )

    def seg(ref, at):
        return ref.at[pl.ds(at * hy, hy)]

    segs = 2 * cx
    swaps = [
        remote(seg(psi, at), seg(partner, at), swap_send.at[at], swap_recv.at[at], {"band": pair})
        for at in range(segs)
    ]

    def planes_out(src, dst, send, recv):
        return [
            remote(seg(src, h * cx + at), dst.at[edge, h], send.at[edge, h], recv.at[edge, h], {"dom": to})
            for edge, at, to in ((0, cx - 1, dom_next), (1, 0, dom_prev))
            for h in range(2)
        ]

    halos = planes_out(psi, halo, halo_send, halo_recv)
    forwards = planes_out(partner, partner_halo, fwd_send, fwd_recv)
    coef_swap = remote(coef.at[0], coef.at[1], pair_send.at[0], pair_recv.at[0], {"band": pair})

    def coef_hop(dist):
        src = coef.at[0] if dist == 1 else coef_below.at[dist - 2]
        return remote(src, coef_below.at[dist - 1], coef_send.at[dist - 1], coef_recv.at[dist - 1], {"band": upper})

    ways = (
        (0, half, from_left, right_send, right_recv, upper, line, left_edges, right_edge_send, right_edge_recv),
        (half, 0, from_right, left_send, left_recv, lower, mirror, right_edges, left_edge_send, left_edge_recv),
    )

    def hop(way, dist, chunk, extra=False):
        base, other, slots, send, recv, target = way[:6]
        if extra:
            src = psi.at[pl.ds(other + chunk * step, step)]
        elif dist == 1:
            src = psi.at[pl.ds(base + chunk * step, step)]
        else:
            src = slots.at[dist - 2, pl.ds(chunk * step, step)]
        return remote(
            src, slots.at[dist - 1, pl.ds(chunk * step, step)],
            send.at[dist - 1, chunk], recv.at[dist - 1, chunk], {"band": target},
        )

    def edge_hops(way, dist):
        other, target, slots, send, recv = way[1], way[5], way[7], way[8], way[9]
        return [
            remote(
                psi.at[other + at * hy] if dist == 1 else slots.at[dist - 2, at],
                slots.at[dist - 1, at], send.at[dist - 1, at], recv.at[dist - 1, at], {"band": target},
            )
            for at in range(cx)
        ]

    def sends(way, dist):
        place = way[6]
        go = (place >= dist - 1) & (place < lines - 1)
        if ends and dist == 1:
            go = go & (place != lines - 2)
        return go

    def sends_extra(way):
        return way[6] == 0

    def receives_edges(way, dist):
        place = way[6]
        got = place >= dist
        if ends and dist == 1:
            got = got & (place != lines - 1)
        return got

    def receives(way, dist):
        place = way[6]
        got = receives_edges(way, dist)
        if ends and dist == 2:
            got = got | (place == 1)
        return got

    outer = sorted({0, cx - 1, cx, segs - 1})
    order = outer + [at for at in range(segs) if at not in outer]
    for copy in halos:
        copy.start()
    for chunk in range(chunks):
        for way in ways:
            @pl.when(sends(way, 1))
            def _(way=way, chunk=chunk):
                hop(way, 1, chunk).start()
    for way in ways:
        @pl.when(sends(way, 1))
        def _(way=way):
            for copy in edge_hops(way, 1):
                copy.start()
    for at in order:
        swaps[at].start()
    if ends:
        for chunk in range(chunks):
            for way in ways:
                @pl.when(sends_extra(way))
                def _(way=way, chunk=chunk):
                    hop(way, 2, chunk, True).start()

    def left_operand(src, edges, first):
        for at in range(segs):
            h, plane = at // cx, at % cx
            opposite = (1 - h) * half + plane * hy

            def body(y, carry, at=at, h=h, plane=plane, opposite=opposite):
                r = at * hy + y
                here = src[r]
                before = edges[0, h, y] if plane == 0 else src[r - hy]
                after = edges[1, h, y] if plane == cx - 1 else src[r + hy]
                beside = before + after
                beside = beside + src[jnp.where(y == 0, opposite + hy - 1, r - 1)]
                beside = beside + src[jnp.where(y == hy - 1, opposite, r + 1)]
                beside = beside + pltpu.roll(here, 1, 1) + pltpu.roll(here, nz - 1, 1)
                hpsi = 0.5 * (6.0 * here - beside) + pot[r] * here
                for slot, value in ((first, hpsi), (first + 1, here)):
                    high, low = parts(value)
                    lhs_high[r, pl.ds(slot * bands, bands)] = high
                    lhs_low[r, pl.ds(slot * bands, bands)] = low
                return carry

            lax.fori_loop(0, hy, body, 0)

    def accumulate(group, source, lhs_row, right_row, count):
        where = pl.ds(group * 2 * bands, 2 * bands)

        def body(k, carry):
            left, right = [], []
            for pos in range(2):
                r = lhs_row + 2 * k + pos
                high, low = lhs_high[r, where], lhs_low[r, where]
                other_high, other_low = parts(right_row(2 * k + pos))
                left += [high, high, low]
                right += [other_high, other_low, other_high]
            out[source, where] += lax.dot_general(
                jnp.concatenate(left, axis=1), jnp.concatenate(right, axis=1), CONTRACT_LAST,
                preferred_element_type=jnp.float32,
            )
            return carry

        lax.fori_loop(0, count // 2, body, 0)

    def moved(way, dist, chunk, group):
        base, other, slots, place = way[0], way[1], way[2], way[6]
        rows_at = base
        if ends and dist == 2:
            rows_at = jnp.where(place == 1, other, base)
        accumulate(
            group, source_of(way, dist), rows_at + chunk * step,
            lambda r: slots[dist - 1, chunk * step + r], step,
        )

    def three(left, right):
        left_high, left_low = left
        right_high, right_low = right
        return lax.dot_general(
            jnp.concatenate([left_high, left_high, left_low], axis=1),
            jnp.concatenate([right_high, right_low, right_high], axis=1),
            CONTRACT_LAST, preferred_element_type=jnp.float32,
        )

    def source_of(way, dist):
        from_place = jnp.maximum(way[6] - dist, 0)
        return from_place if way is ways[0] else lines - 1 - from_place

    def fix_edges(way, dist, group):
        base, other, slots, edges = way[0], way[1], way[2], way[7]
        source = source_of(way, dist)
        where = pl.ds((2 * group + 1) * bands, bands)
        into = pl.ds(2 * group * bands, bands)
        for at in range(cx):
            across = other + at * hy + hy - 1
            last = base + at * hy + hy - 1
            out[source, into] += 0.5 * (
                three((lhs_high[across, where], lhs_low[across, where]), parts(slots[dist - 1, at * hy]))
                - three((lhs_high[last, where], lhs_low[last, where]), parts(edges[dist - 1, at]))
            )

    def corrects(way, dist):
        go = receives_edges(way, dist)
        if ends:
            go = go & (way[6] != 1)
        return go

    def project(source, group, right):
        for kind in range(2):
            coupled = lax.dot_general(
                coef[group], sym[kind], (((1,), (0,)), ((), ())),
                precision=lax.Precision.HIGHEST, preferred_element_type=jnp.float32,
            )
            out[source, pl.ds((2 * group + kind) * bands, bands)] += three(parts(coupled), parts(right))

    out[...] = jnp.zeros_like(out)
    coef[0] = jnp.zeros_like(coef[0])
    for copy in halos:
        copy.wait_recv()
    left_operand(psi, halo, 0)

    def coef_body(r, carry):
        own = pl.ds(bands, bands)
        coef[0] += three((lhs_high[r, own], lhs_low[r, own]), parts(proj[r]))
        return carry

    lax.fori_loop(0, rows, coef_body, 0)
    accumulate(0, line, 0, lambda r: psi[r], rows)
    project(line, 0, coef[0])
    coef_swap.start()

    @pl.when(line < lines - 1)
    def _():
        coef_hop(1).start()

    def start_forwards():
        for at in outer:
            swaps[at].wait_recv()
        for copy in forwards:
            copy.start()

    def pair_start():
        for at in range(segs):
            if at not in outer:
                swaps[at].wait_recv()
        coef_swap.wait_recv()
        for copy in forwards:
            copy.wait_recv()
        left_operand(partner, partner_halo, 2)
        accumulate(1, line, 0, lambda r: psi[r], rows)
        project(line, 1, coef[0])

    def pair_blocks(dist):
        for way in ways:
            @pl.when(receives(way, dist))
            def _(way=way, dist=dist):
                for chunk in range(chunks):
                    moved(way, dist, chunk, 1)

            @pl.when(corrects(way, dist))
            def _(way=way, dist=dist):
                fix_edges(way, dist, 1)

        @pl.when(line >= dist)
        def _(dist=dist):
            project(line - dist, 1, coef_below[dist - 1])

    last = lines - 1
    for dist in range(1, lines):
        if dist == last:
            if last == 1:
                start_forwards()
            pair_start()
            for done in range(1, last):
                pair_blocks(done)
        for chunk in range(chunks):
            for way in ways:
                @pl.when(receives(way, dist))
                def _(way=way, dist=dist, chunk=chunk):
                    hop(way, dist, chunk).wait_recv()

                if dist < lines - 1:
                    @pl.when(sends(way, dist + 1))
                    def _(way=way, dist=dist, chunk=chunk):
                        hop(way, dist + 1, chunk).start()
            for way in ways:
                @pl.when(receives(way, dist))
                def _(way=way, dist=dist, chunk=chunk):
                    moved(way, dist, chunk, 0)
        for way in ways:
            @pl.when(receives_edges(way, dist))
            def _(way=way, dist=dist):
                for copy in edge_hops(way, dist):
                    copy.wait_recv()

            if dist < lines - 1:
                @pl.when(sends(way, dist + 1))
                def _(way=way, dist=dist):
                    for copy in edge_hops(way, dist + 1):
                        copy.start()

            @pl.when(corrects(way, dist))
            def _(way=way, dist=dist):
                fix_edges(way, dist, 0)

        @pl.when(line >= dist)
        def _(dist=dist):
            coef_hop(dist).wait_recv()

        if dist < lines - 1:
            @pl.when((line >= dist) & (line < lines - 1))
            def _(dist=dist):
                coef_hop(dist + 1).start()

        @pl.when(line >= dist)
        def _(dist=dist):
            project(line - dist, 0, coef_below[dist - 1])

        if dist == 1 and last > 1:
            start_forwards()
    pair_blocks(last)

    for copy in swaps + halos + forwards + [coef_swap]:
        copy.wait_send()
    for dist in range(1, lines):
        @pl.when((line >= dist - 1) & (line < lines - 1))
        def _(dist=dist):
            coef_hop(dist).wait_send()

        for way in ways:
            @pl.when(sends(way, dist))
            def _(way=way, dist=dist):
                for copy in edge_hops(way, dist):
                    copy.wait_send()

        for chunk in range(chunks):
            for way in ways:
                go = sends(way, dist)
                if ends and dist == 2:
                    go = go | sends_extra(way)

                @pl.when(go)
                def _(way=way, dist=dist, chunk=chunk):
                    hop(way, dist, chunk).wait_send()


def gram(psi, pot, proj, sym, lines, doms, cx, ny):
    rows, bands, nz = psi.shape
    half = rows // 2
    chunks = 4 if half % 8 == 0 else 1
    hops = lines - 1
    dma = pltpu.SemaphoreType.DMA
    vmem = pl.BlockSpec(memory_space=pltpu.VMEM)
    return pl.pallas_call(
        functools.partial(gram_kernel, lines, doms, cx, ny, chunks),
        out_shape=jax.ShapeDtypeStruct((lines, 4 * bands, bands), jnp.float32),
        in_specs=[vmem] * 4,
        out_specs=vmem,
        scratch_shapes=[
            pltpu.VMEM((rows, bands, nz), jnp.float32),
            pltpu.VMEM((2, 2, ny // 2, bands, nz), jnp.float32),
            pltpu.VMEM((2, 2, ny // 2, bands, nz), jnp.float32),
            pltpu.VMEM((hops, half, bands, nz), jnp.float32),
            pltpu.VMEM((hops, half, bands, nz), jnp.float32),
            pltpu.VMEM((rows, 4 * bands, nz), jnp.bfloat16),
            pltpu.VMEM((rows, 4 * bands, nz), jnp.bfloat16),
            pltpu.VMEM((hops, cx, bands, nz), jnp.float32),
            pltpu.VMEM((hops, cx, bands, nz), jnp.float32),
            pltpu.VMEM((2, bands, proj.shape[1]), jnp.float32),
            pltpu.VMEM((hops, bands, proj.shape[1]), jnp.float32),
            dma((2 * cx,)), dma((2 * cx,)), dma((2, 2)), dma((2, 2)), dma((2, 2)), dma((2, 2)),
            dma((hops, chunks)), dma((hops, chunks)), dma((hops, chunks)), dma((hops, chunks)),
            dma((hops, cx)), dma((hops, cx)), dma((hops, cx)), dma((hops, cx)),
            dma((hops,)), dma((hops,)), dma((1,)), dma((1,)),
        ],
        compiler_params=pltpu.CompilerParams(
            collective_id=0, has_side_effects=True, vmem_limit_bytes=62 * 1024 * 1024
        ),
    )(psi, pot, proj, sym)


def on_device(
    wavefunctions, potential, projectors, hamiltonian_correction, delta_s, projector_count
):
    bands, cx, ny, nz = wavefunctions.shape
    groups = lax.axis_size("band")
    doms = lax.axis_size("dom")
    lines = groups // 2
    mine = lax.axis_index("band")
    line, side = mine // 2, mine % 2
    rows = cx * ny
    volume = 1.0 / (rows * nz * doms)
    hy = ny // 2
    psi = jnp.transpose(wavefunctions.reshape(bands, cx, 2, hy, nz), (2, 1, 3, 0, 4)).reshape(rows, bands, nz)
    pot = jnp.transpose(potential.reshape(cx, 2, hy, nz), (1, 0, 2, 3)).reshape(rows, 1, nz)

    atoms, slots = hamiltonian_correction.shape[:2]
    used = atoms * slots
    width = -(-used // 128) * 128
    mask = (jnp.arange(slots, dtype=jnp.int32)[None, :] < projector_count[:, None]).astype(jnp.float32)
    proj = jnp.transpose(projectors.reshape(used, cx, 2, hy, nz), (2, 1, 3, 0, 4)).reshape(rows, used, nz)
    proj = jnp.pad(proj * mask.reshape(1, used, 1), ((0, 0), (0, width - used), (0, 0)))
    sym = (0.5 / volume) * jnp.stack(
        [
            hamiltonian_correction + jnp.swapaxes(hamiltonian_correction, 1, 2),
            delta_s + jnp.swapaxes(delta_s, 1, 2),
        ]
    )
    same_atom = jnp.eye(atoms, dtype=jnp.float32)[None, :, None, :, None]
    sym = (sym[:, :, :, None, :] * same_atom).reshape(2, used, used)
    sym = jnp.pad(sym, ((0, 0), (0, width - used), (0, width - used)))

    grid = gram(psi, pot, proj, sym, lines, doms, cx, ny)
    here = (jnp.arange(lines, dtype=jnp.int32) == line)[:, None, None, None]
    both = grid.reshape(lines, 4, bands, bands)

    split = 4 % doms == 0
    if split:
        both = lax.all_to_all(both[None], "dom", 2, 0, tiled=True).sum(0)
        first = lax.axis_index("dom") * (4 // doms)
    else:
        both = lax.psum(both, "dom")
        first = 0
    count = both.shape[1]
    lanes = [[at * 2 + s for at in range(lines)] for s in range(2)]
    mirrored = lax.all_to_all(both, "band", 0, 0, axis_index_groups=lanes, tiled=True)
    swapped = lax.ppermute(both, "band", [(i, i ^ 1) for i in range(groups)])
    crossed = ((first + jnp.arange(count, dtype=jnp.int32)) >= 2)[None, :, None, None]
    total = volume * jnp.where(crossed, swapped, both) + volume * jnp.where(here, 0.0, jnp.swapaxes(mirrored, 2, 3))
    if split:
        total = lax.all_gather(total, "dom", axis=1, tiled=True)
    total = total.reshape(lines, 2, 2, bands, bands)
    by_side = jnp.where(side == 0, total, total[:, ::-1])
    final = jnp.transpose(by_side, (2, 3, 0, 1, 4)).reshape(2, bands, groups * bands)
    return final[0], final[1]


def solution(mesh):
    placed = (
        P("band", "dom", None, None),
        P("dom", None, None),
        P("dom", None, None, None, None),
        P("dom", None, None),
        P("dom", None, None),
        P("dom"),
    )
    return jax.shard_map(
        on_device,
        mesh=mesh,
        in_specs=placed,
        out_specs=(P("band", None), P("band", None)),
        check_vma=False,
    )
```

profile of v0, /device:TPU:0, one launch (start us, length us, event | category | flops | bytes accessed | tf_op | source)
XLA Modules:
  0.0 260.0 jit_solution(341012258203306323)
XLA Ops:
  7.2 0.7 fusion.4
  7.9 0.1 reshape.97
  8.0 1.4 copy.50
  9.4 0.9 copy.52
  10.2 0.9 copy.53
  11.1 0.8 fusion.2
  12.0 0.1 mul.48
  12.1 0.1 mul.49
  12.2 0.1 mul.46
  12.3 0.2 mul.47
  12.4 3.0 %copy.51 = f32[72,4,2,8,128]{4,0,3,1,2:T(8,128)S(1)} copy(f32[72,4,2,8,128]{4,3,2,1,0:T(8,128)} %bitcast.43) | data formatting | bytes 4718592 | tf_op jit(solution)/shard_map/reshape | solution.py:444
  15.5 0.7 pad.9.sym
  16.2 0.2 bitcast_multiply_fusion
  16.4 0.0 copy-start
  16.4 2.7 %pad.8.proj = f32[64,128,128]{2,1,0:T(8,128)} pad(f32[64,72,128]{2,1,0:T(8,128)S(1)} %bitcast_multiply_fusion, f32[]{:T(128)} %constant.39.clone.1), padding=0_0x0_56x0_0 | pad | bytes 6553604 | tf_op jit(solution)/shard_map/jit(_pad)/pad | solution.py:445
  19.1 1.0 copy-done
  20.1 4.4 %copy.49 = f32[128,4,2,8,128]{4,0,3,1,2:T(8,128)} copy(f32[128,4,2,8,128]{4,3,2,1,0:T(8,128)S(1)} %bitcast.42) | data formatting | bytes 8388608 | tf_op jit(solution)/shard_map/reshape | solution.py:437
  24.5 169.6 %shard_map.77 = f32[4,512,128]{2,1,0:T(8,128)} custom-call(f32[64,128,128]{2,1,0:T(8,128)} %bitcast.39, f32[64,1,128]{2,1,0:T(1,128)} %bitcast.46, f32[64,128,128]{2,1,0:T(8,128)} %pad.8.proj, f32[2,128,128]{2,1,0:T(8,128)} %pad.9.sym), custom_call_target="tpu_custom_call" | custom-call | tf_op jit(solution)/shard_map/pallas_call | solution.py:397
  194.1 1.3 copy.55
  195.4 17.5 %all_to_all.14 = f32[1,4,4,128,128]{4,3,1,0,2:T(8,128)S(1)} all-to-all(f32[1,4,4,128,128]{4,3,1,0,2:T(8,128)S(1)} %copy.55), channel_id=1, replica_groups=mesh['band'=8,'dom'=4] {'dom'}, dimensions={2} | all-to-all | bytes 2097152 | tf_op jit(solution)/shard_map/all_to_all | solution.py:462
  212.9 0.8 reduce_sum.11
  213.7 8.7 %all-to-all-start.1 = ((f32[4,1,128,128]{3,2,1,0:T(8,128)}), f32[4,1,128,128]{3,2,1,0:T(8,128)S(1)}, u32[]{:S(2)}, u32[]{:S(2)}) async-start(f32[4,1,128,128]{3,2,1,0:T(8,128)} %bitcast.15), calls=%async_computation.1 | async-start | bytes 524288 | tf_op jit(solution)/shard_map/all_to_all | solution.py:469
  222.4 0.0 all-gather.2.cloned.1.call-start
  222.4 1.5 collective-permute-start
  224.0 7.0 %all-to-all-done.1 = f32[4,1,128,128]{3,2,1,0:T(8,128)S(1)} async-done(((f32[4,1,128,128]{3,2,1,0:T(8,128)}), f32[4,1,128,128]{3,2,1,0:T(8,128)S(1)}, u32[]{:S(2)}, u32[]{:S(2)}) %all-to-all-start.1) | async-done | bytes 262176 | tf_op jit(solution)/shard_map/all_to_all | solution.py:469
  230.9 0.1 copy.58
  231.1 0.0 collective-permute-done
  231.1 1.8 fusion.1
  232.8 0.0 all-gather.2.cloned.1.call-update
  232.9 16.4 %all-gather.2.cloned.1.call-done = f32[4,4,128,128]{3,2,0,1:T(8,128)} async-done(((f32[4,1,128,128]{3,2,0,1:T(8,128)}), f32[4,4,128,128]{3,2,0,1:T(8,128)}) %all-gather.2.cloned.1.call-update) | async-done | bytes 1048592 | tf_op jit(solution)/shard_map/all_gather | solution.py:474
  249.2 1.3 copy.59
  250.6 0.1 fusion
  250.7 0.1 fusion.6
  250.7 0.2 copy.61
  250.9 1.0 copy.63
  251.9 0.2 copy.60
  252.1 1.0 copy.62
  (5 shorter events, 0.1 us)
Async XLA Ops:
  16.4 3.7 %copy-start = (f32[128,4,16,128]{3,2,1,0:T(8,128)S(1)}, f32[128,4,16,128]{3,2,1,0:T(8,128)}, u32[]{:S(2)}) copy-start(f32[128,4,16,128]{3,2,1,0:T(8,128)} %param.6) | copy-start | bytes 12582916
  213.7 17.3 %all-to-all-start.1 = ((f32[4,1,128,128]{3,2,1,0:T(8,128)}), f32[4,1,128,128]{3,2,1,0:T(8,128)S(1)}, u32[]{:S(2)}, u32[]{:S(2)}) async-start(f32[4,1,128,128]{3,2,1,0:T(8,128)} %bitcast.15), calls=%async_computation.1 | async-start | bytes 524288 | tf_op jit(solution)/shard_map/all_to_all | solution.py:469
  222.4 26.8 %all-gather.2.cloned.1.call-start = ((), (), s32[]{:S(2)}) async-start(), calls=%async_computation.2 | async-start | bytes 1310720 | tf_op jit(solution)/shard_map/all_gather | solution.py:474
  222.4 8.6 %collective-permute-start = (f32[4,1,128,128]{3,2,0,1:T(8,128)}, f32[4,1,128,128]{3,2,0,1:T(8,128)S(1)}, u32[]{:S(2)}, u32[]{:S(2)}) collective-permute-start(f32[4,1,128,128]{3,2,0,1:T(8,128)} %bitcast.14), channel_id=1, source_target_pairs={{0,4},{4,0},{8,12},{12,8},{16,20},{20,16},{24,28},{28,24},{1,5},{5... | collective-permute-start | bytes 786440 | tf_op jit(solution)/shard_map/ppermute | solution.py:470
Sparse Core Ops, SparseCore 0:
  233.0 16.2 all-gather.1
where the time goes:
time: 261 us; the launch traced here: 260 us
  Pallas kernels  170 us (65%)
  waiting for transfers between devices  23.3 us (9%)
  local copies, waits for them, and re-layouts  20.6 us (8%)
  blocking collectives  17.5 us (7%)
  between operations  14.2 us (5%)
  starting transfers between devices  10.3 us (4%)
  other arithmetic  4.43 us (2%)
    pallas_call x1, Pallas kernels, gram(): pl.pallas_call(functools.partial(gram_kernel, lines, doms, cx, ny, chunks...  170 us
    all_to_all x1, blocking collectives, on_device(): both = lax.all_to_all(both[None], 'dom', 2, 0, tiled=True).sum(0)  17.5 us
    all_gather x1, waiting for transfers between devices, on_device(): total = lax.all_gather(total, 'dom', axis=1, tiled=True)  16.4 us
    all_to_all x1, starting transfers between devices, on_device(): lax.all_to_all(both, 'band', 0, 0, axis_index_groups=lanes, tiled=True)  8.74 us
    all_to_all x1, waiting for transfers between devices, on_device(): lax.all_to_all(both, 'band', 0, 0, axis_index_groups=lanes, tiled=True)  6.97 us
  transfers between devices with their start and end apart: 3, of which 2 were waited for; matrix products, arithmetic and copies ran while one was open for 0% of the time, Pallas kernels for 0%

commit v1 on v0

v1 whole, which is shorter than its diff:
```python
import functools

import jax
import jax.numpy as jnp
from jax import lax
from jax.experimental import pallas as pl
from jax.experimental.pallas import tpu as pltpu
from jax.sharding import PartitionSpec as P

MESH = pl.DeviceIdType.MESH
CONTRACT_LAST = (((1,), (1,)), ((), ()))
MATMUL = (((1,), (0,)), ((), ()))
QUADS = 4


def parts(value):
    high = value.astype(jnp.bfloat16)
    low = (value - high.astype(jnp.float32)).astype(jnp.bfloat16)
    return high, low


def three(left, right, dims, axis):
    (left_high, left_low), (right_high, right_low) = left, right
    return lax.dot_general(
        jnp.concatenate([left_high, left_high, left_low], axis=1),
        jnp.concatenate([right_high, right_low, right_high], axis=axis),
        dims, preferred_element_type=jnp.float32,
    )


def exact(left, right):
    return lax.dot_general(
        left, right, MATMUL, precision=lax.Precision.HIGHEST, preferred_element_type=jnp.float32
    )


def gram_kernel(lines, doms, fused, volume, counts, psi_in, pot, proj_in, ham_corr, delta, result, *scratch):
    (
        nat, packed, partner, halo, partner_halo, slots_r, slots_l, lhs_high, lhs_low,
        own_edge, left_edge, edges_r, edges_l, proj, sym, coef, coef_below, coup_high, coup_low,
        load_sem, proj_sem, swap_send, swap_recv, halo_send, halo_recv, fwd_send, fwd_recv,
        right_send, right_recv, left_send, left_recv,
        right_edge_send, right_edge_recv, left_edge_send, left_edge_recv,
        coef_send, coef_recv, pair_send, pair_recv,
    ) = scratch[:39]
    rows, bands, nz = nat.shape
    cx, ny = pot.shape[:2]
    lane_half = nz // 2
    half = rows // 2
    per_y = cx // 2
    steps = ny // 2
    phases = lines - 2
    hops = lines - 1
    last = lines - 1
    atoms, slots = ham_corr.shape[:2]
    used = atoms * slots
    live = -(-used // 8) * 8
    width = sym.shape[1]
    grid = scratch[39] if fused else result

    mine = lax.axis_index("band")
    dom = lax.axis_index("dom")
    line = mine // 2
    side = mine % 2
    pair = line * 2 + (1 - side)
    upper = jnp.minimum(line + 1, last) * 2 + side
    lower = jnp.maximum(line - 1, 0) * 2 + side
    dom_next = (dom + 1) % doms
    dom_prev = (dom + doms - 1) % doms

    def loads(y):
        copies = []
        for p in range(cx):
            r = y * cx + p
            copies.append(pltpu.make_async_copy(psi_in.at[:, p, y], nat.at[r], load_sem.at[r]))
        return copies

    def proj_loads(y):
        copies = []
        for p in range(cx):
            r = y * cx + p
            copies.append(pltpu.make_async_copy(proj_in.at[:, p, y], proj.at[r], proj_sem.at[r]))
        return copies

    def start_loads(y, carry):
        for copy in loads(y):
            copy.start()
        return carry

    def start_proj(y, carry):
        for copy in proj_loads(y):
            copy.start()
        return carry

    lax.fori_loop(0, ny, start_loads, 0)
    lax.fori_loop(0, ny, start_proj, 0)

    barrier = pltpu.get_barrier_semaphore()
    pl.semaphore_signal(barrier, inc=1, device_id={"band": pair}, device_id_type=MESH)
    for ahead in range(1, lines):
        there = (line + ahead) % lines * 2 + side
        pl.semaphore_signal(barrier, inc=1, device_id={"band": there}, device_id_type=MESH)
    for ahead in range(1, doms):
        pl.semaphore_signal(barrier, inc=1, device_id={"dom": (dom + ahead) % doms}, device_id_type=MESH)
    pl.semaphore_wait(barrier, 1 + hops + doms - 1)

    def remote(src, dst, send, recv, where):
        return pltpu.make_async_remote_copy(
            src_ref=src, dst_ref=dst, send_sem=send, recv_sem=recv,
            device_id=where, device_id_type=MESH,
        )

    def swap(y):
        at = pl.ds(y * cx, cx)
        return remote(nat.at[at], partner.at[at], swap_send.at[y], swap_recv.at[y], {"band": pair})

    def planes(src, dst, send, recv, y):
        return [
            remote(src.at[y * cx + p], dst.at[edge, y], send.at[edge, y], recv.at[edge, y], {"dom": to})
            for edge, p, to in ((0, cx - 1, dom_next), (1, 0, dom_prev))
        ]

    def halos(y):
        return planes(nat, halo, halo_send, halo_recv, y)

    def forwards(y):
        return planes(partner, partner_halo, fwd_send, fwd_recv, y)

    class Way:
        def __init__(self, base, place, slots, edges, send, recv, edge_send, edge_recv, to):
            self.base, self.place, self.slots, self.edges = base, place, slots, edges
            self.send, self.recv, self.edge_send, self.edge_recv, self.to = send, recv, edge_send, edge_recv, to
            self.count = jnp.where(place == 0, 0, jnp.where(place == 1, 2, jnp.where(place == last, last - 1, place)))
            self.own_first = place < last - 1
            self.shift = jnp.where(self.own_first, 1, 0)

        def source(self, f):
            from_place = jnp.where(
                self.place == 1, 0, jnp.where(self.place == last, self.place - 2 - f, self.place - 1 - f)
            )
            from_place = jnp.clip(from_place, 0, last)
            return from_place if self.base == 0 else last - from_place

        def half_of(self, f):
            return jnp.where(self.place == 1, 1 - self.base, self.base) if f == 1 else self.base

        def gets(self, f):
            return self.count > f

        def gets_edge(self, f):
            return (self.count > f) & (self.place != 1) if f else self.count > 0

        def passes(self, f):
            return (self.place >= 1) & (self.place < last) & (self.place > f)

        def own(self, y):
            at = pl.ds(y * per_y, per_y)
            return remote(
                packed.at[self.base, at], self.slots.at[0, at], self.send.at[0, y], self.recv.at[0, y], {"band": self.to}
            )

        def extra(self, y):
            at = pl.ds(y * per_y, per_y)
            return remote(
                packed.at[1 - self.base, at], self.slots.at[1, at], self.send.at[1, y], self.recv.at[1, y],
                {"band": self.to},
            )

        def hop(self, f, y):
            at = pl.ds(y * per_y, per_y)
            q = jnp.minimum(f + self.shift, phases - 1)
            return remote(
                self.slots.at[f, at], self.slots.at[q, at], self.send.at[q, y], self.recv.at[q, y], {"band": self.to}
            )

        def arrival(self, f, y):
            at = pl.ds(y * per_y, per_y)
            return remote(
                self.slots.at[f, at], self.slots.at[f, at], self.send.at[f, y], self.recv.at[f, y], {"band": self.to}
            )

        def own_edge(self):
            return remote(own_edge, self.edges.at[0], self.edge_send.at[0], self.edge_recv.at[0], {"band": self.to})

        def edge_hop(self, f):
            q = jnp.minimum(f + self.shift, phases - 1)
            return remote(
                self.edges.at[f], self.edges.at[q], self.edge_send.at[q], self.edge_recv.at[q], {"band": self.to}
            )

        def edge_arrival(self, f):
            return remote(
                self.edges.at[f], self.edges.at[f], self.edge_send.at[f], self.edge_recv.at[f], {"band": self.to}
            )

    ways = (
        Way(0, line, slots_r, edges_r, right_send, right_recv, right_edge_send, right_edge_recv, upper),
        Way(1, last - line, slots_l, edges_l, left_send, left_recv, left_edge_send, left_edge_recv, lower),
    )
    live_rows = pl.ds(0, live)
    coef_swap = remote(
        coef.at[0, live_rows], coef.at[1, live_rows], pair_send.at[0], pair_recv.at[0], {"band": pair}
    )

    def coef_hop(dist):
        src = coef.at[0, live_rows] if dist == 1 else coef_below.at[dist - 2, live_rows]
        return remote(
            src, coef_below.at[dist - 1, live_rows], coef_send.at[dist - 1], coef_recv.at[dist - 1], {"band": upper}
        )

    lanes = lax.broadcasted_iota(jnp.int32, (bands, nz), 1)
    low_lanes = lanes < lane_half

    def pack(first, second):
        return (
            jnp.where(low_lanes, first, pltpu.roll(second, lane_half, 1)),
            jnp.where(low_lanes, pltpu.roll(first, lane_half, 1), second),
        )

    def start_own(y):
        for way in ways:
            @pl.when(way.own_first)
            def _(way=way):
                way.own(y).start()

    own_edge[...] = jnp.zeros_like(own_edge)
    left_edge[...] = jnp.zeros_like(left_edge)

    def begin(y, carry):
        for copy in loads(y):
            copy.wait()
        swap(y).start()
        for copy in halos(y):
            copy.start()
        for pp in range(per_y):
            k = y * per_y + pp
            first, second = pack(nat[2 * k], nat[2 * k + 1])
            packed[0, k] = first
            packed[1, k] = second

        @pl.when((y >= 1) & (y <= steps))
        def _():
            start_own(y - 1)

        return carry

    lax.fori_loop(0, ny, begin, 0)

    def gather_edge(r, carry):
        here = nat[r]
        spot = (lanes == r) | (lanes == r + lane_half)
        return jnp.where(spot, pltpu.roll(here, (r + lane_half) % nz, 1), carry)

    own_edge[...] = lax.fori_loop(0, rows, gather_edge, jnp.zeros((bands, nz), jnp.float32))

    for kind, source in enumerate((ham_corr, delta)):
        total = jnp.zeros((width, width), jnp.float32)
        for a in range(atoms):
            wide = lax.broadcasted_iota(jnp.int32, (slots, width), 0) + a * slots
            place = wide == lax.broadcasted_iota(jnp.int32, (slots, width), 1)
            place = place & (wide - a * slots < counts[a])
            tall = lax.broadcasted_iota(jnp.int32, (width, slots), 1) + a * slots
            tall_place = tall == lax.broadcasted_iota(jnp.int32, (width, slots), 0)
            tall_place = tall_place & (tall - a * slots < counts[a])
            total = total + exact(tall_place.astype(jnp.float32), exact(source[a], place.astype(jnp.float32)))
        sym[kind] = (0.5 / volume) * (total + jnp.transpose(total))

    coef[0] = jnp.zeros((width, bands), jnp.float32)
    if live < width:
        unused = jnp.zeros((width - live, bands), jnp.float32)
        coef[1, pl.ds(live, width - live)] = unused
        for slot in range(hops):
            coef_below[slot, pl.ds(live, width - live)] = unused

    def coef_body(y, carry):
        for copy in proj_loads(y):
            copy.wait()
        left, right = [], []
        for p in range(cx):
            r = y * cx + p
            proj_high, proj_low = parts(proj[r])
            high, low = parts(nat[r])
            left += [proj_high, proj_high, proj_low]
            right += [high, low, high]
        coef[0, pl.ds(0, used)] += lax.dot_general(
            jnp.concatenate(left, axis=1), jnp.concatenate(right, axis=1), CONTRACT_LAST,
            preferred_element_type=jnp.float32,
        )
        return carry

    lax.fori_loop(0, ny, coef_body, 0)

    for way in ways:
        @pl.when(way.own_first)
        def _(way=way):
            way.own_edge().start()

    coef_swap.start()

    @pl.when(line < last)
    def _():
        coef_hop(1).start()

    def start_rest(y, carry):
        start_own(y)
        return carry

    lax.fori_loop(steps, ny, start_rest, 0)
    for way in ways:
        @pl.when(way.place == 0)
        def _(way=way):
            def body(y, carry):
                way.extra(y).start()
                return carry

            lax.fori_loop(0, ny, body, 0)

    grid[...] = jnp.zeros_like(grid)

    def operand(src, edges, group, y):
        up = (y + ny - 1) % ny
        down = (y + 1) % ny
        edge = left_edge[group]
        for pp in range(per_y):
            k = y * per_y + pp
            hpsi, own = [], []
            for t in range(2):
                p = 2 * pp + t
                r = y * cx + p
                here = src[r]
                before = edges[0, y] if p == 0 else src[r - 1]
                after = edges[1, y] if p == cx - 1 else src[r + 1]
                beside = before + after
                beside = beside + src[up * cx + p]
                beside = beside + src[down * cx + p]
                beside = beside + jnp.where(lanes % lane_half == 0, 0.0, pltpu.roll(here, 1, 1))
                beside = beside + pltpu.roll(here, nz - 1, 1)
                hpsi.append(0.5 * (6.0 * here - beside) + pot[p, pl.ds(y, 1)] * here)
                own.append(here)
                spot = (lanes == r) | (lanes == r + lane_half)
                edge = jnp.where(spot, -0.5 * pltpu.roll(here, (r + lane_half + 1) % nz, 1), edge)
            for slot, both in ((2 * group, pack(*hpsi)), (2 * group + 1, pack(*own))):
                for h in range(2):
                    high, low = parts(both[h])
                    lhs_high[h * half + k, pl.ds(slot * bands, bands)] = high
                    lhs_low[h * half + k, pl.ds(slot * bands, bands)] = low
        left_edge[group] = edge

    def accumulate(group, source, row, right_row, count):
        where = pl.ds(group * 2 * bands, 2 * bands)
        left, right = [], []
        for i in range(count):
            high, low = lhs_high[row + i, where], lhs_low[row + i, where]
            other_high, other_low = right_row(i)
            left += [high, high, low]
            right += [other_high, other_low, other_high]
        grid[source, where] += lax.dot_general(
            jnp.concatenate(left, axis=1), jnp.concatenate(right, axis=1), CONTRACT_LAST,
            preferred_element_type=jnp.float32,
        )

    def with_own(group, y, ys):
        own = pl.ds(bands, bands)
        for h in range(2):
            row = h * half + y * per_y
            accumulate(
                group, line, row, lambda i, row=row: (lhs_high[row + i, own], lhs_low[row + i, own]), ys * per_y
            )

    def with_moved(group, way, f, y, ys):
        accumulate(
            group, way.source(f), way.half_of(f) * half + y * per_y,
            lambda i: parts(way.slots[f, y * per_y + i]), ys * per_y,
        )

    def moved_all(group, f, y, ys):
        for way in ways:
            @pl.when(way.gets(f))
            def _(way=way):
                with_moved(group, way, f, y, ys)

    def take(f, t):
        for y in (2 * t, 2 * t + 1):
            for way in ways:
                @pl.when(way.gets(f))
                def _(way=way, y=y):
                    way.arrival(f, y).wait_recv()

                @pl.when(way.passes(f))
                def _(way=way, y=y):
                    way.hop(f, y).start()

    def partner_operand(y):
        for copy in forwards(y):
            copy.wait_recv()
        operand(partner, partner_halo, 1, y)

    def with_edges(group):
        into = pl.ds(2 * group * bands, bands)
        left = parts(left_edge[group])
        grid[line, into] += three(left, parts(own_edge[...]), CONTRACT_LAST, 1)
        for way in ways:
            for f in range(phases):
                @pl.when(way.gets_edge(f))
                def _(way=way, f=f):
                    keep = (low_lanes if way.base == 0 else ~low_lanes) | (way.place == 1)
                    grid[way.source(f), into] += three(
                        left, parts(jnp.where(keep, way.edges[f], 0.0)), CONTRACT_LAST, 1
                    )

    def edge_stage(f):
        for way in ways:
            @pl.when(way.gets_edge(f))
            def _(way=way):
                way.edge_arrival(f).wait_recv()

            @pl.when(way.passes(f))
            def _(way=way):
                way.edge_hop(f).start()

    def couple(group):
        for kind in range(2):
            coupled = jnp.transpose(exact(sym[kind], coef[group]))
            high, low = parts(coupled)
            where = pl.ds((2 * group + kind) * bands, bands)
            coup_high[where] = high
            coup_low[where] = low

    def project(source, right):
        grid[source] += three((coup_high[...], coup_low[...]), parts(right), MATMUL, 0)

    def coef_stage(dist):
        @pl.when(line >= dist)
        def _():
            coef_hop(dist).wait_recv()

        if dist < hops:
            @pl.when((line >= dist) & (line < last))
            def _():
                coef_hop(dist + 1).start()

        @pl.when(line >= dist)
        def _():
            project(line - dist, coef_below[dist - 1])

    def partner_row(u):
        swap(u).wait_recv()
        for copy in forwards(u):
            copy.start()

        @pl.when(u >= 2)
        def _():
            partner_operand(u - 1)
            with_own(1, u - 1, 1)
            moved_all(1, 0, u - 1, 1)

    def first_phase(t, carry):
        for y in (2 * t, 2 * t + 1):
            for copy in halos(y):
                copy.wait_recv()
            operand(nat, halo, 0, y)
        with_own(0, 2 * t, 2)
        take(0, t)
        moved_all(0, 0, 2 * t, 2)
        partner_row(t)
        return carry

    lax.fori_loop(0, steps, first_phase, 0)

    coef_swap.wait_recv()
    couple(0)
    couple(1)
    project(line, coef[0])
    edge_stage(0)
    coef_stage(1)

    def second_phase(t, carry):
        take(1, t)
        moved_all(0, 1, 2 * t, 2)
        partner_row(steps + t)
        for y in (2 * t, 2 * t + 1):
            @pl.when((y != 0) & (y != ny - 1))
            def _(y=y):
                moved_all(1, 1, y, 1)

        for stage in range(1, hops):
            @pl.when(t == min(2 * stage, steps - 2))
            def _(stage=stage):
                if stage < phases:
                    edge_stage(stage)
                coef_stage(stage + 1)

        @pl.when(t == steps - 2)
        def _():
            with_edges(0)

        return carry

    lax.fori_loop(0, steps, second_phase, 0)
    for y in (0, ny - 1):
        partner_operand(y)
        with_own(1, y, 1)
        moved_all(1, 0, y, 1)
        moved_all(1, 1, y, 1)
    with_edges(1)
    for f in range(2, phases):
        def later_phase(t, carry, f=f):
            take(f, t)
            moved_all(0, f, 2 * t, 2)
            moved_all(1, f, 2 * t, 2)
            return carry

        lax.fori_loop(0, steps, later_phase, 0)

    if fused:
        combine(
            lines, volume, grid, result, remote, line, side, pair, dom, scratch[40:],
        )

    def finish(y, carry):
        swap(y).wait_send()
        for copy in halos(y) + forwards(y):
            copy.wait_send()
        for way in ways:
            @pl.when(way.own_first)
            def _(way=way):
                way.own(y).wait_send()

            @pl.when(way.place == 0)
            def _(way=way):
                way.extra(y).wait_send()

            for f in range(phases):
                @pl.when(way.passes(f))
                def _(way=way, f=f):
                    way.hop(f, y).wait_send()

        return carry

    lax.fori_loop(0, ny, finish, 0)
    coef_swap.wait_send()
    for dist in range(1, lines):
        @pl.when((line >= dist - 1) & (line < last))
        def _(dist=dist):
            coef_hop(dist).wait_send()
    for way in ways:
        @pl.when(way.own_first)
        def _(way=way):
            way.own_edge().wait_send()

        for f in range(phases):
            @pl.when(way.passes(f))
            def _(way=way, f=f):
                way.edge_hop(f).wait_send()


def combine(lines, volume, grid, result, remote, line, side, pair, dom, scratch):
    (
        from_core, both, from_chip, total, mirror, swapped,
        core_send, core_recv, chip_send, chip_recv, line_send, line_recv, side_send, side_recv,
        near_send, near_recv, far_send, far_recv, pass_send, pass_recv,
    ) = scratch
    bands = grid.shape[2]
    core = dom % 2
    kind = dom // 2
    other_core = kind * 2 + (1 - core)
    other_chip = (1 - kind) * 2 + core
    mine = pl.ds(pl.multiple_of(core * 2 * bands, bands), 2 * bands)
    theirs = pl.ds(pl.multiple_of((1 - core) * 2 * bands, bands), 2 * bands)
    my_kind = pl.ds(pl.multiple_of(kind * bands, bands), bands)
    their_kind = pl.ds(pl.multiple_of((1 - kind) * bands, bands), bands)

    def to_core(s):
        return remote(grid.at[s, theirs], from_core.at[s], core_send.at[s], core_recv.at[s], {"dom": other_core})

    def to_chip(s):
        return remote(both.at[s, their_kind], from_chip.at[s], chip_send.at[s], chip_recv.at[s], {"dom": other_chip})

    def to_line(s):
        return remote(
            total.at[s], mirror.at[line], line_send.at[s], line_recv.at[line], {"band": s * 2 + side}
        )

    def from_line(s):
        return remote(
            total.at[s], mirror.at[s], line_send.at[s], line_recv.at[s], {"band": s * 2 + side}
        )

    def to_side(s):
        return remote(total.at[s], swapped.at[s], side_send.at[s], side_recv.at[s], {"band": pair})

    def column(s):
        block = s * 2 + jnp.where(core == 0, side, 1 - side)
        return pl.ds(pl.multiple_of(block * bands, bands), bands)

    def piece(s, k, send, recv, to):
        at = result.at[k, :, column(s)]
        return remote(at, at, send.at[s], recv.at[s], {"dom": to})

    def near(s):
        return piece(s, kind, near_send, near_recv, other_core)

    def near_arrival(s):
        block = s * 2 + jnp.where(core == 1, side, 1 - side)
        at = result.at[kind, :, pl.ds(pl.multiple_of(block * bands, bands), bands)]
        return remote(at, at, near_send.at[s], near_recv.at[s], {"dom": other_core})

    def far(s):
        return piece(s, kind, far_send, far_recv, other_chip)

    def far_arrival(s):
        return piece(s, 1 - kind, far_send, far_recv, other_chip)

    def onward(s):
        return piece(s, 1 - kind, pass_send, pass_recv, other_core)

    def onward_arrival(s):
        block = s * 2 + jnp.where(core == 1, side, 1 - side)
        at = result.at[1 - kind, :, pl.ds(pl.multiple_of(block * bands, bands), bands)]
        return remote(at, at, pass_send.at[s], pass_recv.at[s], {"dom": other_core})

    everyone = range(lines)
    for s in everyone:
        to_core(s).start()
    for s in everyone:
        to_core(s).wait_recv()
        both[s] = grid[s, mine] + from_core[s]
        to_chip(s).start()
    for s in everyone:
        to_chip(s).wait_recv()
        total[s] = both[s, my_kind] + from_chip[s]

        @pl.when(line != s)
        def _(s=s):
            to_line(s).start()

        @pl.when(core == 1)
        def _(s=s):
            to_side(s).start()
    for s in everyone:
        @pl.when(core == 1)
        def _(s=s):
            to_side(s).wait_recv()
            result[kind, :, column(s)] = volume * swapped[s]

        @pl.when(core == 0)
        def _(s=s):
            result[kind, :, column(s)] = volume * total[s]

        @pl.when(line != s)
        def _(s=s):
            from_line(s).wait_recv()
            result[kind, :, column(s)] += volume * jnp.transpose(mirror[s])

        near(s).start()
        far(s).start()
    for s in everyone:
        far_arrival(s).wait_recv()
        onward(s).start()
    for s in everyone:
        near_arrival(s).wait_recv()
        onward_arrival(s).wait_recv()
    for s in everyone:
        to_core(s).wait_send()
        to_chip(s).wait_send()
        near(s).wait_send()
        far(s).wait_send()
        onward(s).wait_send()

        @pl.when(line != s)
        def _(s=s):
            to_line(s).wait_send()

        @pl.when(core == 1)
        def _(s=s):
            to_side(s).wait_send()


def gram(psi, pot, proj, ham_corr, delta, counts, lines, doms, fused, volume):
    bands, cx, ny, nz = psi.shape
    rows = cx * ny
    half = rows // 2
    used = proj.shape[0]
    width = -(-used // 128) * 128
    hops = lines - 1
    phases = lines - 2
    f32 = jnp.float32
    dma = pltpu.SemaphoreType.DMA
    vmem = pl.BlockSpec(memory_space=pltpu.VMEM)
    hbm = pl.BlockSpec(memory_space=pl.ANY)
    scratch = [
        pltpu.VMEM((rows, bands, nz), f32),
        pltpu.VMEM((2, half, bands, nz), f32),
        pltpu.VMEM((rows, bands, nz), f32),
        pltpu.VMEM((2, ny, bands, nz), f32),
        pltpu.VMEM((2, ny, bands, nz), f32),
        pltpu.VMEM((phases, half, bands, nz), f32),
        pltpu.VMEM((phases, half, bands, nz), f32),
        pltpu.VMEM((rows, QUADS * bands, nz), jnp.bfloat16),
        pltpu.VMEM((rows, QUADS * bands, nz), jnp.bfloat16),
        pltpu.VMEM((bands, nz), f32),
        pltpu.VMEM((2, bands, nz), f32),
        pltpu.VMEM((phases, bands, nz), f32),
        pltpu.VMEM((phases, bands, nz), f32),
        pltpu.VMEM((rows, used, nz), f32),
        pltpu.VMEM((2, width, width), f32),
        pltpu.VMEM((2, width, bands), f32),
        pltpu.VMEM((hops, width, bands), f32),
        pltpu.VMEM((QUADS * bands, width), jnp.bfloat16),
        pltpu.VMEM((QUADS * bands, width), jnp.bfloat16),
        dma((rows,)), dma((rows,)), dma((ny,)), dma((ny,)), dma((2, ny)), dma((2, ny)), dma((2, ny)), dma((2, ny)),
        dma((phases, ny)), dma((phases, ny)), dma((phases, ny)), dma((phases, ny)),
        dma((phases,)), dma((phases,)), dma((phases,)), dma((phases,)),
        dma((hops,)), dma((hops,)), dma((1,)), dma((1,)),
    ]
    if fused:
        shape = (2, bands, 2 * lines * bands)
        scratch += [
            pltpu.VMEM((lines, QUADS * bands, bands), f32),
            pltpu.VMEM((lines, 2 * bands, bands), f32),
            pltpu.VMEM((lines, 2 * bands, bands), f32),
            pltpu.VMEM((lines, bands, bands), f32),
            pltpu.VMEM((lines, bands, bands), f32),
            pltpu.VMEM((lines, bands, bands), f32),
            pltpu.VMEM((lines, bands, bands), f32),
        ] + [dma((lines,))] * 14
    else:
        shape = (lines, QUADS * bands, bands)
    return pl.pallas_call(
        functools.partial(gram_kernel, lines, doms, fused, volume),
        out_shape=jax.ShapeDtypeStruct(shape, f32),
        in_specs=[pl.BlockSpec(memory_space=pltpu.SMEM), hbm, vmem, hbm, vmem, vmem],
        out_specs=vmem,
        scratch_shapes=scratch,
        compiler_params=pltpu.CompilerParams(
            collective_id=0, has_side_effects=True, vmem_limit_bytes=62 * 1024 * 1024
        ),
    )(counts, psi, pot, proj, ham_corr, delta)


def on_device(
    wavefunctions, potential, projectors, hamiltonian_correction, delta_s, projector_count
):
    bands, cx, ny, nz = wavefunctions.shape
    groups = lax.axis_size("band")
    doms = lax.axis_size("dom")
    lines = groups // 2
    mine = lax.axis_index("band")
    line, side = mine // 2, mine % 2
    volume = 1.0 / (cx * ny * nz * doms)
    atoms, slots = hamiltonian_correction.shape[:2]
    proj = projectors.reshape(atoms * slots, cx, ny, nz)
    fused = doms == QUADS and bands % 128 == 0
    grid = gram(
        wavefunctions, potential, proj, hamiltonian_correction, delta_s, projector_count,
        lines, doms, fused, volume,
    )
    if fused:
        return grid[0], grid[1]
    here = (jnp.arange(lines, dtype=jnp.int32) == line)[:, None, None, None]
    both = lax.psum(grid.reshape(lines, QUADS, bands, bands), "dom")
    lanes = [[at * 2 + s for at in range(lines)] for s in range(2)]
    mirrored = lax.all_to_all(both, "band", 0, 0, axis_index_groups=lanes, tiled=True)
    swapped = lax.ppermute(both, "band", [(i, i ^ 1) for i in range(groups)])
    crossed = (jnp.arange(QUADS, dtype=jnp.int32) >= 2)[None, :, None, None]
    total = volume * jnp.where(crossed, swapped, both) + volume * jnp.where(here, 0.0, jnp.swapaxes(mirrored, 2, 3))
    total = total.reshape(lines, 2, 2, bands, bands)
    by_side = jnp.where(side == 0, total, total[:, ::-1])
    final = jnp.transpose(by_side, (2, 3, 0, 1, 4)).reshape(2, bands, groups * bands)
    return final[0], final[1]


def solution(mesh):
    placed = (
        P("band", "dom", None, None),
        P("dom", None, None),
        P("dom", None, None, None, None),
        P("dom", None, None),
        P("dom", None, None),
        P("dom"),
    )
    return jax.shard_map(
        on_device,
        mesh=mesh,
        in_specs=placed,
        out_specs=(P("band", None), P("band", None)),
        check_vma=False,
    )
```

time: 261 us -> 185 us (0.71)
  waiting for transfers between devices: 23.3 us -> 0 us
  blocking collectives: 17.5 us -> 0 us
  local copies, waits for them, and re-layouts: 20.6 us -> 5.06 us
  between operations: 14.2 us -> 0.64 us
  starting transfers between devices: 10.3 us -> 0 us
  Pallas kernels: 170 us -> 177 us
  other arithmetic: 4.43 us -> 0 us
    all_to_all x1 -> x0, blocking collectives: 17.5 us -> none  [on_device(): both = lax.all_to_all(both[None], 'dom', 2, 0, tiled=True).sum(0)]
    all_gather x1 -> x0, waiting for transfers between devices: 16.4 us -> none  [on_device(): total = lax.all_gather(total, 'dom', axis=1, tiled=True)]
    reshape x3 -> x0, local copies, waits for them, and re-layouts: 8.79 us -> none  [the longest x1 4.37 us: on_device(): wavefunctions.reshape(bands, cx, 2, hy, nz)]
    all_to_all x1 -> x0, starting transfers between devices: 8.74 us -> none  [on_device(): lax.all_to_all(both, 'band', 0, 0, axis_index_groups=lanes, tiled=True)]
    all_to_all x1 -> x0, waiting for transfers between devices: 6.97 us -> none  [on_device(): lax.all_to_all(both, 'band', 0, 0, axis_index_groups=lanes, tiled=True)]
    pallas_call x1, Pallas kernels: 170 us -> 177 us  [gram(): pl.pallas_call(functools.partial(gram_kernel, lines, doms, fused, volume)...]
    pad x2 -> x0, local copies, waits for them, and re-layouts: 3.34 us -> none  [the longest x1 2.68 us: on_device(): jnp.pad(proj * mask.reshape(1, used, 1), ((0, 0), (0, width - used), (0,...]
  transfers between devices with their start and end apart: 3 -> 0, of which waited for: 2 -> 0; matrix products, arithmetic and copies ran while one was open for 0% -> 0% of each run, Pallas kernels for 0% -> 0%
where the time goes in v1:
time: 185 us; the launch traced here: 182 us
  Pallas kernels  177 us (96%)
  local copies, waits for them, and re-layouts  5.06 us (3%)
    pallas_call x1, Pallas kernels, gram(): pl.pallas_call(functools.partial(gram_kernel, lines, doms, fused, volume)...  177 us

profile of v1, /device:TPU:0, one launch (start us, length us, event | category | flops | bytes accessed | tf_op | source)
XLA Modules:
  0.0 182.3 jit_solution(6714039575857830252)
XLA Ops:
  0.6 1.4 copy.8.ham_corr
  2.0 1.4 copy.9.delta
  3.4 176.6 %shard_map.77 = f32[2,128,1024]{2,1,0:T(8,128)} custom-call(s32[4]{0:T(128)} %counts.1, f32[128,4,16,128]{3,2,1,0:T(8,128)} %psi_in.1, f32[4,16,128]{2,1,0:T(8,128)} %pot.1, f32[72,4,16,128]{3,2,1,0:T(8,128)} %bitcast.5, f32[4,18,18]{2,1,0:T(8,128)} %copy.8.ham_corr, f32[4,18,18]{2,1,0:T(8,128)} %copy.9.delta), custom_call_target="tpu_custom_call" | custom-call | tf_op jit(solution)/shard_map/pallas_call | solution.py:729
  180.0 2.3 %slice_bitcast_fusion = (f32[128,1024]{1,0:T(8,128)}, f32[128,1024]{1,0:T(8,128)}) fusion(f32[2,128,1024]{2,1,0:T(8,128)} %shard_map.77), kind=kLoop, calls=%fused_computation | loop fusion | bytes 2097152 | tf_op jit(solution)/shard_map/squeeze | solution.py:759

commit v2 on v1

--- a/solution.py
+++ b/solution.py
@@ -11,6 +11,9 @@
 CONTRACT_LAST = (((1,), (1,)), ((), ()))
 MATMUL = (((1,), (0,)), ((), ()))
 QUADS = 4
+WINDOW = 8
+SWAP_WINDOW = 4
+HALO_AHEAD = 6
 
 
 def parts(value):
@@ -52,6 +55,9 @@
     phases = lines - 2
     hops = lines - 1
     last = lines - 1
+    window = min(WINDOW, ny)
+    swap_window = min(SWAP_WINDOW, ny)
+    halo_ahead = min(HALO_AHEAD, ny)
     atoms, slots = ham_corr.shape[:2]
     used = atoms * slots
     live = -(-used // 8) * 8
@@ -133,6 +139,7 @@
             self.count = jnp.where(place == 0, 0, jnp.where(place == 1, 2, jnp.where(place == last, last - 1, place)))
             self.own_first = place < last - 1
             self.shift = jnp.where(self.own_first, 1, 0)
+            self.items = jnp.where(place == 0, 2, place + 1) * ny
 
         def source(self, f):
             from_place = jnp.where(
@@ -178,6 +185,36 @@
             return remote(
                 self.slots.at[f, at], self.slots.at[f, at], self.send.at[f, y], self.recv.at[f, y], {"band": self.to}
             )
+
+        def start_item(self, item):
+            q, y = item // ny, item % ny
+
+            @pl.when(q == 0)
+            def _():
+                self.own(y).start()
+
+            @pl.when((q == 1) & (self.place == 0))
+            def _():
+                self.extra(y).start()
+
+            @pl.when((q >= 1) & (self.place >= 1))
+            def _():
+                self.hop(jnp.clip(q - 1, 0, phases - 1), y).start()
+
+        def sent(self, item):
+            q, y = item // ny, item % ny
+            at = pl.ds(y * per_y, per_y)
+            remote(
+                packed.at[self.base, at], self.slots.at[q, at], self.send.at[q, y], self.recv.at[q, y],
+                {"band": self.to},
+            ).wait_send()
+
+        def pace(self, u):
+            for item in (2 * u + window, 2 * u + window + 1):
+                @pl.when(self.own_first & (item < self.items))
+                def _(item=item):
+                    self.sent(item - window)
+                    self.start_item(item)
 
         def own_edge(self):
             return remote(own_edge, self.edges.at[0], self.edge_send.at[0], self.edge_recv.at[0], {"band": self.to})
@@ -229,29 +266,38 @@
     def begin(y, carry):
         for copy in loads(y):
             copy.wait()
-        swap(y).start()
-        for copy in halos(y):
-            copy.start()
+
+        @pl.when(y < swap_window)
+        def _():
+            swap(y).start()
+
+        @pl.when(y < halo_ahead)
+        def _():
+            for copy in halos(y):
+                copy.start()
+
         for pp in range(per_y):
             k = y * per_y + pp
             first, second = pack(nat[2 * k], nat[2 * k + 1])
             packed[0, k] = first
             packed[1, k] = second
 
-        @pl.when((y >= 1) & (y <= steps))
+        @pl.when((y >= 1) & (y <= window))
         def _():
             start_own(y - 1)
 
         return carry
 
     lax.fori_loop(0, ny, begin, 0)
+    if window == ny:
+        start_own(ny - 1)
 
     def gather_edge(r, carry):
         here = nat[r]
         spot = (lanes == r) | (lanes == r + lane_half)
         return jnp.where(spot, pltpu.roll(here, (r + lane_half) % nz, 1), carry)
 
-    own_edge[...] = lax.fori_loop(0, rows, gather_edge, jnp.zeros((bands, nz), jnp.float32))
+    own_edge[...] = lax.fori_loop(0, rows, gather_edge, jnp.zeros((bands, nz), jnp.float32), unroll=8)
 
     for kind, source in enumerate((ham_corr, delta)):
         total = jnp.zeros((width, width), jnp.float32)
@@ -300,20 +346,6 @@
     @pl.when(line < last)
     def _():
         coef_hop(1).start()
-
-    def start_rest(y, carry):
-        start_own(y)
-        return carry
-
-    lax.fori_loop(steps, ny, start_rest, 0)
-    for way in ways:
-        @pl.when(way.place == 0)
-        def _(way=way):
-            def body(y, carry):
-                way.extra(y).start()
-                return carry
-
-            lax.fori_loop(0, ny, body, 0)
 
     grid[...] = jnp.zeros_like(grid)
 
@@ -386,9 +418,12 @@
                 def _(way=way, y=y):
                     way.arrival(f, y).wait_recv()
 
-                @pl.when(way.passes(f))
+                @pl.when(way.passes(f) & (way.shift == 0))
                 def _(way=way, y=y):
                     way.hop(f, y).start()
+
+        for way in ways:
+            way.pace(f * steps + t)
 
     def partner_operand(y):
         for copy in forwards(y):
@@ -448,6 +483,11 @@
         for copy in forwards(u):
             copy.start()
 
+        @pl.when(u + swap_window < ny)
+        def _():
+            swap(u).wait_send()
+            swap(u + swap_window).start()
+
         @pl.when(u >= 2)
         def _():
             partner_operand(u - 1)
@@ -455,6 +495,12 @@
             moved_all(1, 0, u - 1, 1)
 
     def first_phase(t, carry):
+        for y in (halo_ahead + 2 * t, halo_ahead + 2 * t + 1):
+            @pl.when(y < ny)
+            def _(y=y):
+                for copy in halos(y):
+                    copy.start()
+
         for y in (2 * t, 2 * t + 1):
             for copy in halos(y):
                 copy.wait_recv()
@@ -518,20 +564,19 @@
         )
 
     def finish(y, carry):
-        swap(y).wait_send()
+        @pl.when(y >= ny - swap_window)
+        def _():
+            swap(y).wait_send()
+
         for copy in halos(y) + forwards(y):
             copy.wait_send()
         for way in ways:
-            @pl.when(way.own_first)
+            @pl.when(way.own_first & (y < window))
             def _(way=way):
-                way.own(y).wait_send()
-
-            @pl.when(way.place == 0)
-            def _(way=way):
-                way.extra(y).wait_send()
+                way.sent(way.items - window + y)
 
             for f in range(phases):
-                @pl.when(way.passes(f))
+                @pl.when(way.passes(f) & (way.shift == 0))
                 def _(way=way, f=f):
                     way.hop(f, y).wait_send()
 

time: 185 us -> 146 us (0.79)
  Pallas kernels: 177 us -> 138 us
    pallas_call x1, Pallas kernels: 177 us -> 138 us  [gram(): pl.pallas_call(functools.partial(gram_kernel, lines, doms, fused, volume)...]
where the time goes in v2:
time: 146 us; the launch traced here: 144 us
  Pallas kernels  138 us (95%)
  local copies, waits for them, and re-layouts  5.06 us (3%)
    pallas_call x1, Pallas kernels, gram(): pl.pallas_call(functools.partial(gram_kernel, lines, doms, fused, volume)...  138 us

profile of v2, /device:TPU:0, one launch (start us, length us, event | category | flops | bytes accessed | tf_op | source)
XLA Modules:
  0.0 143.7 jit_solution(12936953353990974333)
XLA Ops:
  0.6 1.4 copy.8.ham_corr
  2.0 1.4 copy.9.delta
  3.4 138.0 %shard_map.77 = f32[2,128,1024]{2,1,0:T(8,128)} custom-call(s32[4]{0:T(128)} %counts.1, f32[128,4,16,128]{3,2,1,0:T(8,128)} %psi_in.1, f32[4,16,128]{2,1,0:T(8,128)} %pot.1, f32[72,4,16,128]{3,2,1,0:T(8,128)} %bitcast.5, f32[4,18,18]{2,1,0:T(8,128)} %copy.8.ham_corr, f32[4,18,18]{2,1,0:T(8,128)} %copy.9.delta), custom_call_target="tpu_custom_call" | custom-call | tf_op jit(solution)/shard_map/pallas_call | solution.py:774
  141.4 2.3 %slice_bitcast_fusion = (f32[128,1024]{1,0:T(8,128)}, f32[128,1024]{1,0:T(8,128)}) fusion(f32[2,128,1024]{2,1,0:T(8,128)} %shard_map.77), kind=kLoop, calls=%fused_computation | loop fusion | bytes 2097152 | tf_op jit(solution)/shard_map/squeeze | solution.py:804

commit v3 on v2

--- a/solution.py
+++ b/solution.py
@@ -37,15 +37,22 @@
     )
 
 
-def gram_kernel(lines, doms, fused, volume, counts, psi_in, pot, proj_in, ham_corr, delta, result, *scratch):
+def remote(src, dst, send, recv, where):
+    return pltpu.make_async_remote_copy(
+        src_ref=src, dst_ref=dst, send_sem=send, recv_sem=recv,
+        device_id=where, device_id_type=MESH,
+    )
+
+
+def gram_kernel(lines, doms, fused, volume, counts, psi_in, pot, proj_in, corrections, result, *scratch):
     (
         nat, packed, partner, halo, partner_halo, slots_r, slots_l, lhs_high, lhs_low,
-        own_edge, left_edge, edges_r, edges_l, proj, sym, coef, coef_below, coup_high, coup_low,
+        own_edge, full_edge, left_edge, edges_r, edges_l, proj, sym, coef, coef_below, coup_high, coup_low,
         load_sem, proj_sem, swap_send, swap_recv, halo_send, halo_recv, fwd_send, fwd_recv,
         right_send, right_recv, left_send, left_recv,
         right_edge_send, right_edge_recv, left_edge_send, left_edge_recv,
         coef_send, coef_recv, pair_send, pair_recv,
-    ) = scratch[:39]
+    ) = scratch[:40]
     rows, bands, nz = nat.shape
     cx, ny = pot.shape[:2]
     lane_half = nz // 2
@@ -58,11 +65,11 @@
     window = min(WINDOW, ny)
     swap_window = min(SWAP_WINDOW, ny)
     halo_ahead = min(HALO_AHEAD, ny)
-    atoms, slots = ham_corr.shape[:2]
+    atoms, slots = corrections.shape[1:3]
     used = atoms * slots
     live = -(-used // 8) * 8
     width = sym.shape[1]
-    grid = scratch[39] if fused else result
+    grid = scratch[40] if fused else result
 
     mine = lax.axis_index("band")
     dom = lax.axis_index("dom")
@@ -98,23 +105,25 @@
             copy.start()
         return carry
 
+    if fused:
+        combine = Combine(lines, volume, grid, result, line, side, pair, dom, scratch[41:])
     lax.fori_loop(0, ny, start_loads, 0)
     lax.fori_loop(0, ny, start_proj, 0)
 
     barrier = pltpu.get_barrier_semaphore()
     pl.semaphore_signal(barrier, inc=1, device_id={"band": pair}, device_id_type=MESH)
-    for ahead in range(1, lines):
-        there = (line + ahead) % lines * 2 + side
-        pl.semaphore_signal(barrier, inc=1, device_id={"band": there}, device_id_type=MESH)
+
+    @pl.when(line > 0)
+    def _():
+        pl.semaphore_signal(barrier, inc=1, device_id={"band": lower}, device_id_type=MESH)
+
+    @pl.when(line < last)
+    def _():
+        pl.semaphore_signal(barrier, inc=1, device_id={"band": upper}, device_id_type=MESH)
+
     for ahead in range(1, doms):
         pl.semaphore_signal(barrier, inc=1, device_id={"dom": (dom + ahead) % doms}, device_id_type=MESH)
-    pl.semaphore_wait(barrier, 1 + hops + doms - 1)
-
-    def remote(src, dst, send, recv, where):
-        return pltpu.make_async_remote_copy(
-            src_ref=src, dst_ref=dst, send_sem=send, recv_sem=recv,
-            device_id=where, device_id_type=MESH,
-        )
+    pl.semaphore_wait(barrier, doms + jnp.minimum(line, 1) + jnp.minimum(last - line, 1))
 
     def swap(y):
         at = pl.ds(y * cx, cx)
@@ -154,9 +163,6 @@
         def gets(self, f):
             return self.count > f
 
-        def gets_edge(self, f):
-            return (self.count > f) & (self.place != 1) if f else self.count > 0
-
         def passes(self, f):
             return (self.place >= 1) & (self.place < last) & (self.place > f)
 
@@ -217,7 +223,15 @@
                     self.start_item(item)
 
         def own_edge(self):
-            return remote(own_edge, self.edges.at[0], self.edge_send.at[0], self.edge_recv.at[0], {"band": self.to})
+            return remote(
+                own_edge.at[self.base], self.edges.at[0], self.edge_send.at[0], self.edge_recv.at[0], {"band": self.to}
+            )
+
+        def extra_edge(self):
+            return remote(
+                own_edge.at[1 - self.base], self.edges.at[1], self.edge_send.at[1], self.edge_recv.at[1],
+                {"band": self.to},
+            )
 
         def edge_hop(self, f):
             q = jnp.minimum(f + self.shift, phases - 1)
@@ -249,9 +263,10 @@
     low_lanes = lanes < lane_half
 
     def pack(first, second):
+        low = low_lanes[: first.shape[0]]
         return (
-            jnp.where(low_lanes, first, pltpu.roll(second, lane_half, 1)),
-            jnp.where(low_lanes, pltpu.roll(first, lane_half, 1), second),
+            jnp.where(low, first, pltpu.roll(second, lane_half, 1)),
+            jnp.where(low, pltpu.roll(first, lane_half, 1), second),
         )
 
     def start_own(y):
@@ -260,7 +275,6 @@
             def _(way=way):
                 way.own(y).start()
 
-    own_edge[...] = jnp.zeros_like(own_edge)
     left_edge[...] = jnp.zeros_like(left_edge)
 
     def begin(y, carry):
@@ -297,9 +311,12 @@
         spot = (lanes == r) | (lanes == r + lane_half)
         return jnp.where(spot, pltpu.roll(here, (r + lane_half) % nz, 1), carry)
 
-    own_edge[...] = lax.fori_loop(0, rows, gather_edge, jnp.zeros((bands, nz), jnp.float32), unroll=8)
-
-    for kind, source in enumerate((ham_corr, delta)):
+    edge = lax.fori_loop(0, rows, gather_edge, jnp.zeros((bands, nz), jnp.float32), unroll=8)
+    full_edge[...] = edge
+    for h, value in enumerate(pack(edge[: bands // 2], edge[bands // 2 :])):
+        own_edge[h] = value
+
+    for kind in range(2):
         total = jnp.zeros((width, width), jnp.float32)
         for a in range(atoms):
             wide = lax.broadcasted_iota(jnp.int32, (slots, width), 0) + a * slots
@@ -308,7 +325,7 @@
             tall = lax.broadcasted_iota(jnp.int32, (width, slots), 1) + a * slots
             tall_place = tall == lax.broadcasted_iota(jnp.int32, (width, slots), 0)
             tall_place = tall_place & (tall - a * slots < counts[a])
-            total = total + exact(tall_place.astype(jnp.float32), exact(source[a], place.astype(jnp.float32)))
+            total = total + exact(tall_place.astype(jnp.float32), exact(corrections[kind, a], place.astype(jnp.float32)))
         sym[kind] = (0.5 / volume) * (total + jnp.transpose(total))
 
     coef[0] = jnp.zeros((width, bands), jnp.float32)
@@ -340,6 +357,10 @@
         @pl.when(way.own_first)
         def _(way=way):
             way.own_edge().start()
+
+        @pl.when(way.place == 0)
+        def _(way=way):
+            way.extra_edge().start()
 
     coef_swap.start()
 
@@ -433,19 +454,27 @@
     def with_edges(group):
         into = pl.ds(2 * group * bands, bands)
         left = parts(left_edge[group])
-        grid[line, into] += three(left, parts(own_edge[...]), CONTRACT_LAST, 1)
+        grid[line, into] += three(left, parts(full_edge[...]), CONTRACT_LAST, 1)
         for way in ways:
             for f in range(phases):
-                @pl.when(way.gets_edge(f))
+                @pl.when(way.gets(f))
                 def _(way=way, f=f):
-                    keep = (low_lanes if way.base == 0 else ~low_lanes) | (way.place == 1)
-                    grid[way.source(f), into] += three(
-                        left, parts(jnp.where(keep, way.edges[f], 0.0)), CONTRACT_LAST, 1
+                    low = low_lanes[: bands // 2] ^ (way.half_of(f) == 1)
+                    here = way.edges[f]
+                    turned = pltpu.roll(here, lane_half, 1)
+                    first = way.half_of(f) == 0
+                    right = jnp.concatenate(
+                        [
+                            jnp.where(low, jnp.where(first, here, turned), 0.0),
+                            jnp.where(low, jnp.where(first, turned, here), 0.0),
+                        ],
+                        axis=0,
                     )
+                    grid[way.source(f), into] += three(left, parts(right), CONTRACT_LAST, 1)
 
     def edge_stage(f):
         for way in ways:
-            @pl.when(way.gets_edge(f))
+            @pl.when(way.gets(f))
             def _(way=way):
                 way.edge_arrival(f).wait_recv()
 
@@ -478,7 +507,7 @@
         def _():
             project(line - dist, coef_below[dist - 1])
 
-    def partner_row(u):
+    def partner_row(u, carry):
         swap(u).wait_recv()
         for copy in forwards(u):
             copy.start()
@@ -493,6 +522,8 @@
             partner_operand(u - 1)
             with_own(1, u - 1, 1)
             moved_all(1, 0, u - 1, 1)
+
+        return carry
 
     def first_phase(t, carry):
         for y in (halo_ahead + 2 * t, halo_ahead + 2 * t + 1):
@@ -508,7 +539,7 @@
         with_own(0, 2 * t, 2)
         take(0, t)
         moved_all(0, 0, 2 * t, 2)
-        partner_row(t)
+        partner_row(t, 0)
         return carry
 
     lax.fori_loop(0, steps, first_phase, 0)
@@ -520,35 +551,44 @@
     edge_stage(0)
     coef_stage(1)
 
+    lead_from = steps // 2
+
     def second_phase(t, carry):
         take(1, t)
         moved_all(0, 1, 2 * t, 2)
-        partner_row(steps + t)
+        first = steps + t + jnp.where(t > lead_from, 1, 0)
+        end = steps + t + 1 + jnp.where(t >= lead_from, 1, 0)
+        lax.fori_loop(first, end, partner_row, 0)
         for y in (2 * t, 2 * t + 1):
-            @pl.when((y != 0) & (y != ny - 1))
+            @pl.when(y != 0)
             def _(y=y):
                 moved_all(1, 1, y, 1)
 
         for stage in range(1, hops):
-            @pl.when(t == min(2 * stage, steps - 2))
+            @pl.when(t == min(2 * stage, steps - 3))
             def _(stage=stage):
                 if stage < phases:
                     edge_stage(stage)
                 coef_stage(stage + 1)
 
-        @pl.when(t == steps - 2)
+        @pl.when(t == steps - 3)
         def _():
             with_edges(0)
 
         return carry
 
-    lax.fori_loop(0, steps, second_phase, 0)
+    lax.fori_loop(0, steps - 1, second_phase, 0)
     for y in (0, ny - 1):
         partner_operand(y)
         with_own(1, y, 1)
         moved_all(1, 0, y, 1)
-        moved_all(1, 1, y, 1)
     with_edges(1)
+    take(1, steps - 1)
+    moved_all(0, 1, ny - 2, 2)
+    if fused and phases == 2:
+        combine.send(0)
+    moved_all(1, 1, ny - 2, 2)
+    moved_all(1, 1, 0, 1)
     for f in range(2, phases):
         def later_phase(t, carry, f=f):
             take(f, t)
@@ -559,9 +599,10 @@
         lax.fori_loop(0, steps, later_phase, 0)
 
     if fused:
-        combine(
-            lines, volume, grid, result, remote, line, side, pair, dom, scratch[40:],
-        )
+        if phases > 2:
+            combine.send(0)
+        combine.send(1)
+        combine.rest()
 
     def finish(y, carry):
         @pl.when(y >= ny - swap_window)
@@ -593,135 +634,129 @@
         def _(way=way):
             way.own_edge().wait_send()
 
+        @pl.when(way.place == 0)
+        def _(way=way):
+            way.extra_edge().wait_send()
+
         for f in range(phases):
             @pl.when(way.passes(f))
             def _(way=way, f=f):
                 way.edge_hop(f).wait_send()
 
 
-def combine(lines, volume, grid, result, remote, line, side, pair, dom, scratch):
-    (
-        from_core, both, from_chip, total, mirror, swapped,
-        core_send, core_recv, chip_send, chip_recv, line_send, line_recv, side_send, side_recv,
-        near_send, near_recv, far_send, far_recv, pass_send, pass_recv,
-    ) = scratch
-    bands = grid.shape[2]
-    core = dom % 2
-    kind = dom // 2
-    other_core = kind * 2 + (1 - core)
-    other_chip = (1 - kind) * 2 + core
-    mine = pl.ds(pl.multiple_of(core * 2 * bands, bands), 2 * bands)
-    theirs = pl.ds(pl.multiple_of((1 - core) * 2 * bands, bands), 2 * bands)
-    my_kind = pl.ds(pl.multiple_of(kind * bands, bands), bands)
-    their_kind = pl.ds(pl.multiple_of((1 - kind) * bands, bands), bands)
-
-    def to_core(s):
-        return remote(grid.at[s, theirs], from_core.at[s], core_send.at[s], core_recv.at[s], {"dom": other_core})
-
-    def to_chip(s):
-        return remote(both.at[s, their_kind], from_chip.at[s], chip_send.at[s], chip_recv.at[s], {"dom": other_chip})
-
-    def to_line(s):
-        return remote(
-            total.at[s], mirror.at[line], line_send.at[s], line_recv.at[line], {"band": s * 2 + side}
-        )
-
-    def from_line(s):
-        return remote(
-            total.at[s], mirror.at[s], line_send.at[s], line_recv.at[s], {"band": s * 2 + side}
-        )
-
-    def to_side(s):
-        return remote(total.at[s], swapped.at[s], side_send.at[s], side_recv.at[s], {"band": pair})
-
-    def column(s):
-        block = s * 2 + jnp.where(core == 0, side, 1 - side)
-        return pl.ds(pl.multiple_of(block * bands, bands), bands)
-
-    def piece(s, k, send, recv, to):
-        at = result.at[k, :, column(s)]
-        return remote(at, at, send.at[s], recv.at[s], {"dom": to})
-
-    def near(s):
-        return piece(s, kind, near_send, near_recv, other_core)
-
-    def near_arrival(s):
-        block = s * 2 + jnp.where(core == 1, side, 1 - side)
-        at = result.at[kind, :, pl.ds(pl.multiple_of(block * bands, bands), bands)]
-        return remote(at, at, near_send.at[s], near_recv.at[s], {"dom": other_core})
-
-    def far(s):
-        return piece(s, kind, far_send, far_recv, other_chip)
-
-    def far_arrival(s):
-        return piece(s, 1 - kind, far_send, far_recv, other_chip)
-
-    def onward(s):
-        return piece(s, 1 - kind, pass_send, pass_recv, other_core)
-
-    def onward_arrival(s):
-        block = s * 2 + jnp.where(core == 1, side, 1 - side)
-        at = result.at[1 - kind, :, pl.ds(pl.multiple_of(block * bands, bands), bands)]
-        return remote(at, at, pass_send.at[s], pass_recv.at[s], {"dom": other_core})
-
-    everyone = range(lines)
-    for s in everyone:
-        to_core(s).start()
-    for s in everyone:
-        to_core(s).wait_recv()
-        both[s] = grid[s, mine] + from_core[s]
-        to_chip(s).start()
-    for s in everyone:
-        to_chip(s).wait_recv()
-        total[s] = both[s, my_kind] + from_chip[s]
-
-        @pl.when(line != s)
-        def _(s=s):
-            to_line(s).start()
-
-        @pl.when(core == 1)
-        def _(s=s):
-            to_side(s).start()
-    for s in everyone:
-        @pl.when(core == 1)
-        def _(s=s):
-            to_side(s).wait_recv()
-            result[kind, :, column(s)] = volume * swapped[s]
-
-        @pl.when(core == 0)
-        def _(s=s):
-            result[kind, :, column(s)] = volume * total[s]
-
-        @pl.when(line != s)
-        def _(s=s):
-            from_line(s).wait_recv()
-            result[kind, :, column(s)] += volume * jnp.transpose(mirror[s])
-
-        near(s).start()
-        far(s).start()
-    for s in everyone:
-        far_arrival(s).wait_recv()
-        onward(s).start()
-    for s in everyone:
-        near_arrival(s).wait_recv()
-        onward_arrival(s).wait_recv()
-    for s in everyone:
-        to_core(s).wait_send()
-        to_chip(s).wait_send()
-        near(s).wait_send()
-        far(s).wait_send()
-        onward(s).wait_send()
-
-        @pl.when(line != s)
-        def _(s=s):
-            to_line(s).wait_send()
-
-        @pl.when(core == 1)
-        def _(s=s):
-            to_side(s).wait_send()
-
-
-def gram(psi, pot, proj, ham_corr, delta, counts, lines, doms, fused, volume):
+class Combine:
+    def __init__(self, lines, volume, grid, result, line, side, pair, dom, scratch):
+        (
+            from_core, both, from_chip, total, mirror, swapped,
+            core_send, core_recv, chip_send, chip_recv, line_send, line_recv, side_send, side_recv,
+            near_send, near_recv, far_send, far_recv, pass_send, pass_recv,
+        ) = scratch
+        bands = grid.shape[2]
+        core = dom % 2
+        kind = dom // 2
+        other_core = kind * 2 + (1 - core)
+        other_chip = (1 - kind) * 2 + core
+        my_kind = pl.ds(pl.multiple_of(kind * bands, bands), bands)
+        their_kind = pl.ds(pl.multiple_of((1 - kind) * bands, bands), bands)
+        order = [(line + ahead) % lines for ahead in range(1, lines)] + [line]
+
+        def rows(group):
+            return pl.ds(group * 2 * bands, 2 * bands)
+
+        def to_core(group, s):
+            return remote(
+                grid.at[s, rows(group)], from_core.at[s], core_send.at[s], core_recv.at[s], {"dom": other_core}
+            )
+
+        def to_chip(s):
+            return remote(both.at[s, their_kind], from_chip.at[s], chip_send.at[s], chip_recv.at[s], {"dom": other_chip})
+
+        def to_line(s):
+            return remote(
+                total.at[s], mirror.at[line], line_send.at[s], line_recv.at[line], {"band": s * 2 + side}
+            )
+
+        def from_line(s):
+            return remote(
+                total.at[s], mirror.at[s], line_send.at[s], line_recv.at[s], {"band": s * 2 + side}
+            )
+
+        def to_side(s):
+            return remote(total.at[s], swapped.at[s], side_send.at[s], side_recv.at[s], {"band": pair})
+
+        def piece(s, group, k, send, recv, to):
+            block = s * 2 + (side if group == 0 else 1 - side)
+            at = result.at[k, :, pl.ds(pl.multiple_of(block * bands, bands), bands)]
+            return remote(at, at, send.at[s], recv.at[s], {"dom": to})
+
+        def near(s, group):
+            return piece(s, group, kind, near_send, near_recv, other_core)
+
+        def far(s, group, k):
+            return piece(s, group, k, far_send, far_recv, other_chip)
+
+        def onward(s, group):
+            return piece(s, group, 1 - kind, pass_send, pass_recv, other_core)
+
+        def send(group):
+            @pl.when(core == 1 - group)
+            def _():
+                for s in order:
+                    to_core(group, s).start()
+
+        def work(group):
+            for s in order:
+                to_core(group, s).wait_recv()
+                both[s] = grid[s, rows(group)] + from_core[s]
+                to_chip(s).start()
+            for s in order:
+                to_chip(s).wait_recv()
+                total[s] = both[s, my_kind] + from_chip[s]
+                if s is not line:
+                    to_line(s).start()
+                if group:
+                    to_side(s).start()
+            for s in order:
+                if group:
+                    to_side(s).wait_recv()
+                    value = swapped[s]
+                else:
+                    value = total[s]
+                if s is not line:
+                    from_line(s).wait_recv()
+                    value = value + jnp.transpose(mirror[s])
+                block = s * 2 + (side if group == 0 else 1 - side)
+                result[kind, :, pl.ds(pl.multiple_of(block * bands, bands), bands)] = volume * value
+                far(s, group, kind).start()
+                near(s, group).start()
+            for s in order:
+                far(s, group, 1 - kind).wait_recv()
+                onward(s, group).start()
+            for s in order:
+                near(s, 1 - group).wait_recv()
+                onward(s, 1 - group).wait_recv()
+            for s in order:
+                to_core(1 - group, s).wait_send()
+                to_chip(s).wait_send()
+                near(s, group).wait_send()
+                far(s, group, kind).wait_send()
+                onward(s, group).wait_send()
+                if s is not line:
+                    to_line(s).wait_send()
+                if group:
+                    to_side(s).wait_send()
+
+        def rest():
+            for group in range(2):
+                @pl.when(core == group)
+                def _(group=group):
+                    work(group)
+
+        self.send = send
+        self.rest = rest
+
+
+def gram(psi, pot, proj, corrections, counts, lines, doms, fused, volume):
     bands, cx, ny, nz = psi.shape
     rows = cx * ny
     half = rows // 2
@@ -743,10 +778,11 @@
         pltpu.VMEM((phases, half, bands, nz), f32),
         pltpu.VMEM((rows, QUADS * bands, nz), jnp.bfloat16),
         pltpu.VMEM((rows, QUADS * bands, nz), jnp.bfloat16),
+        pltpu.VMEM((2, bands // 2, nz), f32),
         pltpu.VMEM((bands, nz), f32),
         pltpu.VMEM((2, bands, nz), f32),
-        pltpu.VMEM((phases, bands, nz), f32),
-        pltpu.VMEM((phases, bands, nz), f32),
+        pltpu.VMEM((phases, bands // 2, nz), f32),
+        pltpu.VMEM((phases, bands // 2, nz), f32),
         pltpu.VMEM((rows, used, nz), f32),
         pltpu.VMEM((2, width, width), f32),
         pltpu.VMEM((2, width, bands), f32),
@@ -774,13 +810,13 @@
     return pl.pallas_call(
         functools.partial(gram_kernel, lines, doms, fused, volume),
         out_shape=jax.ShapeDtypeStruct(shape, f32),
-        in_specs=[pl.BlockSpec(memory_space=pltpu.SMEM), hbm, vmem, hbm, vmem, vmem],
+        in_specs=[pl.BlockSpec(memory_space=pltpu.SMEM), hbm, vmem, hbm, vmem],
         out_specs=vmem,
         scratch_shapes=scratch,
         compiler_params=pltpu.CompilerParams(
             collective_id=0, has_side_effects=True, vmem_limit_bytes=62 * 1024 * 1024
         ),
-    )(counts, psi, pot, proj, ham_corr, delta)
+    )(counts, psi, pot, proj, corrections)
 
 
 def on_device(
@@ -797,7 +833,7 @@
     proj = projectors.reshape(atoms * slots, cx, ny, nz)
     fused = doms == QUADS and bands % 128 == 0
     grid = gram(
-        wavefunctions, potential, proj, hamiltonian_correction, delta_s, projector_count,
+        wavefunctions, potential, proj, jnp.stack([hamiltonian_correction, delta_s]), projector_count,
         lines, doms, fused, volume,
     )
     if fused:

time: 146 us -> 140 us (0.959); the launches traced: 144 us -> 139 us
  Pallas kernels: 138 us -> 135 us
  local copies, waits for them, and re-layouts: 5.06 us -> 3.08 us
    pallas_call x1, Pallas kernels: 138 us -> 135 us  [gram(): pl.pallas_call(functools.partial(gram_kernel, lines, doms, fused, volume)...]
    unnamed x2 -> x0, local copies, waits for them, and re-layouts: 2.78 us -> none
where the time goes in v3:
time: 140 us; the launch traced here: 139 us
  Pallas kernels  135 us (96%)
  local copies, waits for them, and re-layouts  3.08 us (2%)
    pallas_call x1, Pallas kernels, gram(): pl.pallas_call(functools.partial(gram_kernel, lines, doms, fused, volume)...  135 us

profile of v3, /device:TPU:0, one launch (start us, length us, event | category | flops | bytes accessed | tf_op | source)
XLA Modules:
  0.0 139.2 jit_solution(16966774270715065500)
XLA Ops:
  0.6 0.8 copy_bitcast_fusion
  1.4 0.7 pad_maximum_fusion.corrections
  2.1 134.9 %shard_map.77 = f32[2,128,1024]{2,1,0:T(8,128)} custom-call(s32[4]{0:T(128)} %counts.1, f32[128,4,16,128]{3,2,1,0:T(8,128)} %psi_in.1, f32[4,16,128]{2,1,0:T(8,128)} %pot.1, f32[72,4,16,128]{3,2,1,0:T(8,128)} %bitcast.9, f32[2,4,18,18]{3,2,1,0:T(8,128)} %pad_maximum_fusion.corrections), custom_call_target="tpu_custom_call" | custom-call | tf_op jit(solution)/shard_map/pallas_call | solution.py:810
  137.0 2.3 %slice_bitcast_fusion = (f32[128,1024]{1,0:T(8,128)}, f32[128,1024]{1,0:T(8,128)}) fusion(f32[2,128,1024]{2,1,0:T(8,128)} %shard_map.77), kind=kLoop, calls=%fused_computation | loop fusion | bytes 2097152 | tf_op jit(solution)/shard_map/squeeze | solution.py:840

commit v4 on v3

--- a/solution.py
+++ b/solution.py
@@ -11,8 +11,8 @@
 CONTRACT_LAST = (((1,), (1,)), ((), ()))
 MATMUL = (((1,), (0,)), ((), ()))
 QUADS = 4
-WINDOW = 8
-SWAP_WINDOW = 4
+WINDOW = 4
+SWAP_WINDOW = 3
 HALO_AHEAD = 6
 
 
@@ -44,7 +44,8 @@
     )
 
 
-def gram_kernel(lines, doms, fused, volume, counts, psi_in, pot, proj_in, corrections, result, *scratch):
+def gram_kernel(lines, doms, fused, volume, counts, psi_in, pot, proj_in, ham_corr, delta, *scratch):
+    result, scratch = scratch[0], scratch[1:]
     (
         nat, packed, partner, halo, partner_halo, slots_r, slots_l, lhs_high, lhs_low,
         own_edge, full_edge, left_edge, edges_r, edges_l, proj, sym, coef, coef_below, coup_high, coup_low,
@@ -65,7 +66,7 @@
     window = min(WINDOW, ny)
     swap_window = min(SWAP_WINDOW, ny)
     halo_ahead = min(HALO_AHEAD, ny)
-    atoms, slots = corrections.shape[1:3]
+    slots, atoms = ham_corr.shape[:2]
     used = atoms * slots
     live = -(-used // 8) * 8
     width = sym.shape[1]
@@ -85,14 +86,14 @@
         copies = []
         for p in range(cx):
             r = y * cx + p
-            copies.append(pltpu.make_async_copy(psi_in.at[:, p, y], nat.at[r], load_sem.at[r]))
+            copies.append(pltpu.make_async_copy(psi_in.at[:, p, y], nat.at[r], load_sem.at[y]))
         return copies
 
     def proj_loads(y):
         copies = []
         for p in range(cx):
             r = y * cx + p
-            copies.append(pltpu.make_async_copy(proj_in.at[:, p, y], proj.at[r], proj_sem.at[r]))
+            copies.append(pltpu.make_async_copy(proj_in.at[:, p, y], proj.at[r], proj_sem.at[0]))
         return copies
 
     def start_loads(y, carry):
@@ -127,13 +128,16 @@
 
     def swap(y):
         at = pl.ds(y * cx, cx)
-        return remote(nat.at[at], partner.at[at], swap_send.at[y], swap_recv.at[y], {"band": pair})
+        return remote(nat.at[at], partner.at[at], swap_send.at[y % swap_window], swap_recv.at[y], {"band": pair})
 
     def planes(src, dst, send, recv, y):
         return [
-            remote(src.at[y * cx + p], dst.at[edge, y], send.at[edge, y], recv.at[edge, y], {"dom": to})
+            remote(src.at[y * cx + p], dst.at[edge, y], send.at[0], recv.at[y], {"dom": to})
             for edge, p, to in ((0, cx - 1, dom_next), (1, 0, dom_prev))
         ]
+
+    def both_planes(dst, send, recv, y):
+        return remote(dst.at[:, y], dst.at[:, y], send.at[0], recv.at[y], {"dom": dom_next})
 
     def halos(y):
         return planes(nat, halo, halo_send, halo_recv, y)
@@ -169,27 +173,29 @@
         def own(self, y):
             at = pl.ds(y * per_y, per_y)
             return remote(
-                packed.at[self.base, at], self.slots.at[0, at], self.send.at[0, y], self.recv.at[0, y], {"band": self.to}
+                packed.at[self.base, at], self.slots.at[0, at], self.send.at[y % window], self.recv.at[0, y],
+                {"band": self.to},
             )
 
         def extra(self, y):
             at = pl.ds(y * per_y, per_y)
             return remote(
-                packed.at[1 - self.base, at], self.slots.at[1, at], self.send.at[1, y], self.recv.at[1, y],
+                packed.at[1 - self.base, at], self.slots.at[1, at], self.send.at[(ny + y) % window], self.recv.at[1, y],
                 {"band": self.to},
             )
 
         def hop(self, f, y):
             at = pl.ds(y * per_y, per_y)
             q = jnp.minimum(f + self.shift, phases - 1)
-            return remote(
-                self.slots.at[f, at], self.slots.at[q, at], self.send.at[q, y], self.recv.at[q, y], {"band": self.to}
+            slot = jnp.where(self.own_first, (q * ny + y) % window, window)
+            return remote(
+                self.slots.at[f, at], self.slots.at[q, at], self.send.at[slot], self.recv.at[q, y], {"band": self.to}
             )
 
         def arrival(self, f, y):
             at = pl.ds(y * per_y, per_y)
             return remote(
-                self.slots.at[f, at], self.slots.at[f, at], self.send.at[f, y], self.recv.at[f, y], {"band": self.to}
+                self.slots.at[f, at], self.slots.at[f, at], self.send.at[0], self.recv.at[f, y], {"band": self.to}
             )
 
         def start_item(self, item):
@@ -211,16 +217,15 @@
             q, y = item // ny, item % ny
             at = pl.ds(y * per_y, per_y)
             remote(
-                packed.at[self.base, at], self.slots.at[q, at], self.send.at[q, y], self.recv.at[q, y],
+                packed.at[self.base, at], self.slots.at[q, at], self.send.at[item % window], self.recv.at[q, y],
                 {"band": self.to},
             ).wait_send()
 
-        def pace(self, u):
-            for item in (2 * u + window, 2 * u + window + 1):
-                @pl.when(self.own_first & (item < self.items))
-                def _(item=item):
-                    self.sent(item - window)
-                    self.start_item(item)
+        def pace(self, item):
+            @pl.when(self.own_first & (item < self.items))
+            def _():
+                self.sent(item - window)
+                self.start_item(item)
 
         def own_edge(self):
             return remote(
@@ -269,6 +274,19 @@
             jnp.where(low, pltpu.roll(first, lane_half, 1), second),
         )
 
+    def take(f, y):
+        for way in ways:
+            @pl.when(way.gets(f))
+            def _(way=way):
+                way.arrival(f, y).wait_recv()
+
+            @pl.when(way.passes(f) & (way.shift == 0))
+            def _(way=way):
+                way.hop(f, y).start()
+
+        for way in ways:
+            way.pace(f * ny + y + window)
+
     def start_own(y):
         for way in ways:
             @pl.when(way.own_first)
@@ -278,8 +296,8 @@
     left_edge[...] = jnp.zeros_like(left_edge)
 
     def begin(y, carry):
-        for copy in loads(y):
-            copy.wait()
+        at = pl.ds(y * cx, cx)
+        pltpu.make_async_copy(nat.at[at], nat.at[at], load_sem.at[y]).wait()
 
         @pl.when(y < swap_window)
         def _():
@@ -316,7 +334,8 @@
     for h, value in enumerate(pack(edge[: bands // 2], edge[bands // 2 :])):
         own_edge[h] = value
 
-    for kind in range(2):
+    take(0, 0)
+    for kind, source in enumerate((ham_corr, delta)):
         total = jnp.zeros((width, width), jnp.float32)
         for a in range(atoms):
             wide = lax.broadcasted_iota(jnp.int32, (slots, width), 0) + a * slots
@@ -325,7 +344,7 @@
             tall = lax.broadcasted_iota(jnp.int32, (width, slots), 1) + a * slots
             tall_place = tall == lax.broadcasted_iota(jnp.int32, (width, slots), 0)
             tall_place = tall_place & (tall - a * slots < counts[a])
-            total = total + exact(tall_place.astype(jnp.float32), exact(corrections[kind, a], place.astype(jnp.float32)))
+            total = total + exact(tall_place.astype(jnp.float32), exact(source[:, a], place.astype(jnp.float32)))
         sym[kind] = (0.5 / volume) * (total + jnp.transpose(total))
 
     coef[0] = jnp.zeros((width, bands), jnp.float32)
@@ -336,8 +355,6 @@
             coef_below[slot, pl.ds(live, width - live)] = unused
 
     def coef_body(y, carry):
-        for copy in proj_loads(y):
-            copy.wait()
         left, right = [], []
         for p in range(cx):
             r = y * cx + p
@@ -351,7 +368,11 @@
         )
         return carry
 
-    lax.fori_loop(0, ny, coef_body, 0)
+    pltpu.make_async_copy(proj, proj, proj_sem.at[0]).wait()
+    lax.fori_loop(0, ny // 2, coef_body, 0)
+    take(0, 1)
+    lax.fori_loop(ny // 2, ny, coef_body, 0)
+    take(0, 2)
 
     for way in ways:
         @pl.when(way.own_first)
@@ -432,45 +453,30 @@
             def _(way=way):
                 with_moved(group, way, f, y, ys)
 
-    def take(f, t):
-        for y in (2 * t, 2 * t + 1):
-            for way in ways:
-                @pl.when(way.gets(f))
-                def _(way=way, y=y):
-                    way.arrival(f, y).wait_recv()
-
-                @pl.when(way.passes(f) & (way.shift == 0))
-                def _(way=way, y=y):
-                    way.hop(f, y).start()
-
-        for way in ways:
-            way.pace(f * steps + t)
-
     def partner_operand(y):
-        for copy in forwards(y):
-            copy.wait_recv()
+        both_planes(partner_halo, fwd_send, fwd_recv, y).wait_recv()
         operand(partner, partner_halo, 1, y)
 
     def with_edges(group):
         into = pl.ds(2 * group * bands, bands)
-        left = parts(left_edge[group])
-        grid[line, into] += three(left, parts(full_edge[...]), CONTRACT_LAST, 1)
+        low = low_lanes[: bands // 2]
+        right = [full_edge[...]]
+        found = []
         for way in ways:
             for f in range(phases):
-                @pl.when(way.gets(f))
-                def _(way=way, f=f):
-                    low = low_lanes[: bands // 2] ^ (way.half_of(f) == 1)
-                    here = way.edges[f]
-                    turned = pltpu.roll(here, lane_half, 1)
-                    first = way.half_of(f) == 0
-                    right = jnp.concatenate(
-                        [
-                            jnp.where(low, jnp.where(first, here, turned), 0.0),
-                            jnp.where(low, jnp.where(first, turned, here), 0.0),
-                        ],
-                        axis=0,
-                    )
-                    grid[way.source(f), into] += three(left, parts(right), CONTRACT_LAST, 1)
+                here = way.edges[f]
+                turned = pltpu.roll(here, lane_half, 1)
+                first = way.half_of(f) == 0
+                keep = (low ^ (way.half_of(f) == 1)) & way.gets(f)
+                right.append(jnp.where(keep, jnp.where(first, here, turned), 0.0))
+                right.append(jnp.where(keep, jnp.where(first, turned, here), 0.0))
+                found.append((way, f))
+        added = three(parts(left_edge[group]), parts(jnp.concatenate(right, axis=0)), CONTRACT_LAST, 1)
+        grid[line, into] += added[:, :bands]
+        for at, (way, f) in enumerate(found):
+            @pl.when(way.gets(f))
+            def _(way=way, f=f, at=at):
+                grid[way.source(f), into] += added[:, (at + 1) * bands : (at + 2) * bands]
 
     def edge_stage(f):
         for way in ways:
@@ -532,12 +538,23 @@
                 for copy in halos(y):
                     copy.start()
 
+        @pl.when(t >= 2)
+        def _():
+            take(0, 2 * t)
+
         for y in (2 * t, 2 * t + 1):
-            for copy in halos(y):
-                copy.wait_recv()
+            both_planes(halo, halo_send, halo_recv, y).wait_recv()
             operand(nat, halo, 0, y)
         with_own(0, 2 * t, 2)
-        take(0, t)
+
+        @pl.when(t >= 2)
+        def _():
+            take(0, 2 * t + 1)
+
+        @pl.when(t == 0)
+        def _():
+            take(0, 3)
+
         moved_all(0, 0, 2 * t, 2)
         partner_row(t, 0)
         return carry
@@ -551,21 +568,18 @@
     edge_stage(0)
     coef_stage(1)
 
-    lead_from = steps // 2
-
     def second_phase(t, carry):
-        take(1, t)
+        take(1, 2 * t)
+        partner_row(steps + t, 0)
+        take(1, 2 * t + 1)
         moved_all(0, 1, 2 * t, 2)
-        first = steps + t + jnp.where(t > lead_from, 1, 0)
-        end = steps + t + 1 + jnp.where(t >= lead_from, 1, 0)
-        lax.fori_loop(first, end, partner_row, 0)
         for y in (2 * t, 2 * t + 1):
             @pl.when(y != 0)
             def _(y=y):
                 moved_all(1, 1, y, 1)
 
         for stage in range(1, hops):
-            @pl.when(t == min(2 * stage, steps - 3))
+            @pl.when(t == min(2 * stage + 1, steps - 3))
             def _(stage=stage):
                 if stage < phases:
                     edge_stage(stage)
@@ -578,20 +592,28 @@
         return carry
 
     lax.fori_loop(0, steps - 1, second_phase, 0)
-    for y in (0, ny - 1):
-        partner_operand(y)
-        with_own(1, y, 1)
-        moved_all(1, 0, y, 1)
+    take(1, ny - 2)
+    partner_row(ny - 1, 0)
+    partner_operand(0)
+    with_own(1, 0, 1)
+    moved_all(1, 0, 0, 1)
+    moved_all(1, 1, 0, 1)
+    take(1, ny - 1)
+    moved_all(0, 1, ny - 2, 2)
+    early = fused and phases == 2
+    if early:
+        combine.send(0)
+    partner_operand(ny - 1)
+    with_own(1, ny - 1, 1)
+    moved_all(1, 0, ny - 1, 1)
+    if early:
+        combine.reduce(0)
+    moved_all(1, 1, ny - 2, 2)
     with_edges(1)
-    take(1, steps - 1)
-    moved_all(0, 1, ny - 2, 2)
-    if fused and phases == 2:
-        combine.send(0)
-    moved_all(1, 1, ny - 2, 2)
-    moved_all(1, 1, 0, 1)
     for f in range(2, phases):
         def later_phase(t, carry, f=f):
-            take(f, t)
+            take(f, 2 * t)
+            take(f, 2 * t + 1)
             moved_all(0, f, 2 * t, 2)
             moved_all(1, f, 2 * t, 2)
             return carry
@@ -599,31 +621,29 @@
         lax.fori_loop(0, steps, later_phase, 0)
 
     if fused:
-        if phases > 2:
+        if not early:
             combine.send(0)
+            combine.reduce(0)
         combine.send(1)
+        combine.reduce(1)
         combine.rest()
 
-    def finish(y, carry):
-        @pl.when(y >= ny - swap_window)
-        def _():
-            swap(y).wait_send()
-
-        for copy in halos(y) + forwards(y):
-            copy.wait_send()
-        for way in ways:
-            @pl.when(way.own_first & (y < window))
-            def _(way=way):
-                way.sent(way.items - window + y)
-
-            for f in range(phases):
-                @pl.when(way.passes(f) & (way.shift == 0))
-                def _(way=way, f=f):
-                    way.hop(f, y).wait_send()
-
-        return carry
-
-    lax.fori_loop(0, ny, finish, 0)
+    for y in range(ny - swap_window, ny):
+        swap(y).wait_send()
+    remote(halo, halo, halo_send.at[0], halo_recv.at[0], {"dom": dom_next}).wait_send()
+    remote(partner_halo, partner_halo, fwd_send.at[0], fwd_recv.at[0], {"dom": dom_next}).wait_send()
+    for way in ways:
+        @pl.when(way.own_first)
+        def _(way=way):
+            for ahead in range(window):
+                way.sent(way.items - window + ahead)
+
+        @pl.when(way.place == last - 1)
+        def _(way=way):
+            remote(
+                way.slots, way.slots, way.send.at[window], way.recv.at[0, 0], {"band": way.to}
+            ).wait_send()
+
     coef_swap.wait_send()
     for dist in range(1, lines):
         @pl.when((line >= dist - 1) & (line < last))
@@ -645,11 +665,11 @@
 
 
 class Combine:
-    def __init__(self, lines, volume, grid, result, line, side, pair, dom, scratch):
+    def __init__(self, lines, volume, grid, out, line, side, pair, dom, scratch):
         (
             from_core, both, from_chip, total, mirror, swapped,
             core_send, core_recv, chip_send, chip_recv, line_send, line_recv, side_send, side_recv,
-            near_send, near_recv, far_send, far_recv, pass_send, pass_recv,
+            near_send, near_recv, far_send, far_recv, pass_send, pass_recv, result, out_sem,
         ) = scratch
         bands = grid.shape[2]
         core = dom % 2
@@ -665,29 +685,29 @@
 
         def to_core(group, s):
             return remote(
-                grid.at[s, rows(group)], from_core.at[s], core_send.at[s], core_recv.at[s], {"dom": other_core}
+                grid.at[s, rows(group)], from_core.at[s], core_send.at[0], core_recv.at[s], {"dom": other_core}
             )
 
         def to_chip(s):
-            return remote(both.at[s, their_kind], from_chip.at[s], chip_send.at[s], chip_recv.at[s], {"dom": other_chip})
+            return remote(both.at[s, their_kind], from_chip.at[s], chip_send.at[0], chip_recv.at[s], {"dom": other_chip})
 
         def to_line(s):
             return remote(
-                total.at[s], mirror.at[line], line_send.at[s], line_recv.at[line], {"band": s * 2 + side}
+                total.at[s], mirror.at[line], line_send.at[0], line_recv.at[line], {"band": s * 2 + side}
             )
 
         def from_line(s):
             return remote(
-                total.at[s], mirror.at[s], line_send.at[s], line_recv.at[s], {"band": s * 2 + side}
+                total.at[s], mirror.at[s], line_send.at[0], line_recv.at[s], {"band": s * 2 + side}
             )
 
         def to_side(s):
-            return remote(total.at[s], swapped.at[s], side_send.at[s], side_recv.at[s], {"band": pair})
+            return remote(total.at[s], swapped.at[s], side_send.at[0], side_recv.at[s], {"band": pair})
 
         def piece(s, group, k, send, recv, to):
             block = s * 2 + (side if group == 0 else 1 - side)
             at = result.at[k, :, pl.ds(pl.multiple_of(block * bands, bands), bands)]
-            return remote(at, at, send.at[s], recv.at[s], {"dom": to})
+            return remote(at, at, send.at[0], recv.at[s], {"dom": to})
 
         def near(s, group):
             return piece(s, group, kind, near_send, near_recv, other_core)
@@ -704,11 +724,20 @@
                 for s in order:
                     to_core(group, s).start()
 
+        def flush(s, group, k):
+            block = s * 2 + (side if group == 0 else 1 - side)
+            at = (k, slice(None), pl.ds(pl.multiple_of(block * bands, bands), bands))
+            pltpu.make_async_copy(result.at[at], out.at[at], out_sem.at[0]).start()
+
+        def reduce(group):
+            @pl.when(core == group)
+            def _():
+                for s in order:
+                    to_core(group, s).wait_recv()
+                    both[s] = grid[s, rows(group)] + from_core[s]
+                    to_chip(s).start()
+
         def work(group):
-            for s in order:
-                to_core(group, s).wait_recv()
-                both[s] = grid[s, rows(group)] + from_core[s]
-                to_chip(s).start()
             for s in order:
                 to_chip(s).wait_recv()
                 total[s] = both[s, my_kind] + from_chip[s]
@@ -729,22 +758,26 @@
                 result[kind, :, pl.ds(pl.multiple_of(block * bands, bands), bands)] = volume * value
                 far(s, group, kind).start()
                 near(s, group).start()
+                flush(s, group, kind)
+            for s in order:
+                near(s, 1 - group).wait_recv()
+                flush(s, 1 - group, kind)
             for s in order:
                 far(s, group, 1 - kind).wait_recv()
                 onward(s, group).start()
+                flush(s, group, 1 - kind)
             for s in order:
-                near(s, 1 - group).wait_recv()
                 onward(s, 1 - group).wait_recv()
-            for s in order:
-                to_core(1 - group, s).wait_send()
-                to_chip(s).wait_send()
-                near(s, group).wait_send()
-                far(s, group, kind).wait_send()
-                onward(s, group).wait_send()
-                if s is not line:
-                    to_line(s).wait_send()
-                if group:
-                    to_side(s).wait_send()
+                flush(s, 1 - group, 1 - kind)
+            pltpu.make_async_copy(result, result, out_sem.at[0]).wait()
+            for held, send, recv in (
+                (from_core, core_send, core_recv), (from_chip, chip_send, chip_recv),
+                (mirror.at[pl.ds(0, lines - 1)], line_send, line_recv), (total, near_send, near_recv),
+                (total, far_send, far_recv), (total, pass_send, pass_recv),
+            ):
+                remote(held, held, send.at[0], recv.at[0], {"dom": other_core}).wait_send()
+            if group:
+                remote(swapped, swapped, side_send.at[0], side_recv.at[0], {"dom": other_core}).wait_send()
 
         def rest():
             for group in range(2):
@@ -753,10 +786,11 @@
                     work(group)
 
         self.send = send
+        self.reduce = reduce
         self.rest = rest
 
 
-def gram(psi, pot, proj, corrections, counts, lines, doms, fused, volume):
+def gram(psi, pot, proj, ham_corr, delta, counts, lines, doms, fused, volume):
     bands, cx, ny, nz = psi.shape
     rows = cx * ny
     half = rows // 2
@@ -764,6 +798,7 @@
     width = -(-used // 128) * 128
     hops = lines - 1
     phases = lines - 2
+    window = min(WINDOW, ny) + 1
     f32 = jnp.float32
     dma = pltpu.SemaphoreType.DMA
     vmem = pl.BlockSpec(memory_space=pltpu.VMEM)
@@ -789,13 +824,15 @@
         pltpu.VMEM((hops, width, bands), f32),
         pltpu.VMEM((QUADS * bands, width), jnp.bfloat16),
         pltpu.VMEM((QUADS * bands, width), jnp.bfloat16),
-        dma((rows,)), dma((rows,)), dma((ny,)), dma((ny,)), dma((2, ny)), dma((2, ny)), dma((2, ny)), dma((2, ny)),
-        dma((phases, ny)), dma((phases, ny)), dma((phases, ny)), dma((phases, ny)),
+        dma((ny,)), dma((1,)), dma((min(SWAP_WINDOW, ny),)), dma((ny,)), dma((1,)), dma((ny,)), dma((1,)), dma((ny,)),
+        dma((window,)), dma((phases, ny)), dma((window,)), dma((phases, ny)),
         dma((phases,)), dma((phases,)), dma((phases,)), dma((phases,)),
         dma((hops,)), dma((hops,)), dma((1,)), dma((1,)),
     ]
     if fused:
-        shape = (2, bands, 2 * lines * bands)
+        columns = 2 * lines * bands
+        shape = jax.ShapeDtypeStruct((2, bands, columns), f32)
+        placed = hbm
         scratch += [
             pltpu.VMEM((lines, QUADS * bands, bands), f32),
             pltpu.VMEM((lines, 2 * bands, bands), f32),
@@ -804,19 +841,20 @@
             pltpu.VMEM((lines, bands, bands), f32),
             pltpu.VMEM((lines, bands, bands), f32),
             pltpu.VMEM((lines, bands, bands), f32),
-        ] + [dma((lines,))] * 14
+        ] + [dma((1,)), dma((lines,))] * 7 + [pltpu.VMEM((2, bands, columns), f32), dma((1,))]
     else:
-        shape = (lines, QUADS * bands, bands)
+        shape = jax.ShapeDtypeStruct((lines, QUADS * bands, bands), f32)
+        placed = vmem
     return pl.pallas_call(
         functools.partial(gram_kernel, lines, doms, fused, volume),
-        out_shape=jax.ShapeDtypeStruct(shape, f32),
-        in_specs=[pl.BlockSpec(memory_space=pltpu.SMEM), hbm, vmem, hbm, vmem],
-        out_specs=vmem,
+        out_shape=shape,
+        in_specs=[pl.BlockSpec(memory_space=pltpu.SMEM), hbm, vmem, hbm, vmem, vmem],
+        out_specs=placed,
         scratch_shapes=scratch,
         compiler_params=pltpu.CompilerParams(
             collective_id=0, has_side_effects=True, vmem_limit_bytes=62 * 1024 * 1024
         ),
-    )(counts, psi, pot, proj, corrections)
+    )(counts, psi, pot, proj, ham_corr, delta)
 
 
 def on_device(
@@ -833,8 +871,8 @@
     proj = projectors.reshape(atoms * slots, cx, ny, nz)
     fused = doms == QUADS and bands % 128 == 0
     grid = gram(
-        wavefunctions, potential, proj, jnp.stack([hamiltonian_correction, delta_s]), projector_count,
-        lines, doms, fused, volume,
+        wavefunctions, potential, proj, jnp.transpose(hamiltonian_correction, (1, 0, 2)),
+        jnp.transpose(delta_s, (1, 0, 2)), projector_count, lines, doms, fused, volume,
     )
     if fused:
         return grid[0], grid[1]

time: 140 us -> 130 us (0.929); the launches traced: 139 us -> 128 us
  Pallas kernels: 135 us -> 125 us
    pallas_call x1, Pallas kernels: 135 us -> 125 us  [gram(): pl.pallas_call(functools.partial(gram_kernel, lines, doms, fused, volume)...]
where the time goes in v4:
time: 130 us; the launch traced here: 128 us
  Pallas kernels  125 us (96%)
  local copies, waits for them, and re-layouts  2.28 us (2%)
    pallas_call x1, Pallas kernels, gram(): pl.pallas_call(functools.partial(gram_kernel, lines, doms, fused, volume)...  125 us

profile of v4, /device:TPU:0, one launch (start us, length us, event | category | flops | bytes accessed | tf_op | source)
XLA Modules:
  0.0 127.8 jit_solution(3523741143061624754)
XLA Ops:
  0.6 124.9 %shard_map.77 = f32[2,128,1024]{2,1,0:T(8,128)} custom-call(s32[4]{0:T(128)} %counts.1, f32[128,4,16,128]{3,2,1,0:T(8,128)} %psi_in.1, f32[4,16,128]{2,1,0:T(8,128)} %pot.1, f32[72,4,16,128]{3,2,1,0:T(8,128)} %bitcast.7, f32[18,4,18]{2,1,0:T(4,128)} %bitcast.8, f32[18,4,18]{2,1,0:T(4,128)} %bitcast.9), custom_call_target="tpu_custom_call" | custom-call | tf_op jit(solution)/shard_map/pallas_call | solution.py:848
  125.5 2.3 %slice_bitcast_fusion = (f32[128,1024]{1,0:T(8,128)}, f32[128,1024]{1,0:T(8,128)}) fusion(f32[2,128,1024]{2,1,0:T(8,128)} %shard_map.77), kind=kLoop, calls=%fused_computation | loop fusion | bytes 2097152 | tf_op jit(solution)/shard_map/squeeze | solution.py:878

commit v5 on v4

--- a/solution.py
+++ b/solution.py
@@ -12,7 +12,7 @@
 MATMUL = (((1,), (0,)), ((), ()))
 QUADS = 4
 WINDOW = 4
-SWAP_WINDOW = 3
+SWAP_WINDOW = 4
 HALO_AHEAD = 6
 
 
@@ -276,16 +276,18 @@
 
     def take(f, y):
         for way in ways:
-            @pl.when(way.gets(f))
+            @pl.when(way.passes(f) & (way.shift == 0))
             def _(way=way):
                 way.arrival(f, y).wait_recv()
-
-            @pl.when(way.passes(f) & (way.shift == 0))
-            def _(way=way):
                 way.hop(f, y).start()
 
         for way in ways:
             way.pace(f * ny + y + window)
+
+        for way in ways:
+            @pl.when(way.gets(f) & ~(way.passes(f) & (way.shift == 0)))
+            def _(way=way):
+                way.arrival(f, y).wait_recv()
 
     def start_own(y):
         for way in ways:
@@ -592,13 +594,23 @@
         return carry
 
     lax.fori_loop(0, steps - 1, second_phase, 0)
+    between = (line > 0) & (line < last)
     take(1, ny - 2)
     partner_row(ny - 1, 0)
+
+    @pl.when(between)
+    def _():
+        take(1, ny - 1)
+
     partner_operand(0)
     with_own(1, 0, 1)
     moved_all(1, 0, 0, 1)
     moved_all(1, 1, 0, 1)
-    take(1, ny - 1)
+
+    @pl.when(~between)
+    def _():
+        take(1, ny - 1)
+
     moved_all(0, 1, ny - 2, 2)
     early = fused and phases == 2
     if early:
@@ -678,7 +690,10 @@
         other_chip = (1 - kind) * 2 + core
         my_kind = pl.ds(pl.multiple_of(kind * bands, bands), bands)
         their_kind = pl.ds(pl.multiple_of((1 - kind) * bands, bands), bands)
-        order = [(line + ahead) % lines for ahead in range(1, lines)] + [line]
+        turn = jnp.where(line == 0, 1, 0)
+        others = [(line + 1 + (k + turn) % (lines - 1)) % lines for k in range(lines - 1)]
+        order = others + [line]
+        closing = [line] + others
 
         def rows(group):
             return pl.ds(group * 2 * bands, 2 * bands)
@@ -745,7 +760,7 @@
                     to_line(s).start()
                 if group:
                     to_side(s).start()
-            for s in order:
+            for s in closing:
                 if group:
                     to_side(s).wait_recv()
                     value = swapped[s]
@@ -759,14 +774,14 @@
                 far(s, group, kind).start()
                 near(s, group).start()
                 flush(s, group, kind)
-            for s in order:
+            for s in closing:
                 near(s, 1 - group).wait_recv()
                 flush(s, 1 - group, kind)
-            for s in order:
+            for s in closing:
                 far(s, group, 1 - kind).wait_recv()
                 onward(s, group).start()
                 flush(s, group, 1 - kind)
-            for s in order:
+            for s in closing:
                 onward(s, 1 - group).wait_recv()
                 flush(s, 1 - group, 1 - kind)
             pltpu.make_async_copy(result, result, out_sem.at[0]).wait()

time: 130 us -> 129 us (level); the launches traced: 128 us -> 129 us
  no operation moved by 1% of the time
where the time goes in v5:
time: 129 us
  Pallas kernels  126 us (98%)
  local copies, waits for them, and re-layouts  2.28 us (2%)
    pallas_call x1, Pallas kernels, gram(): pl.pallas_call(functools.partial(gram_kernel, lines, doms, fused, volume)...  126 us

profile of v5, /device:TPU:0, one launch (start us, length us, event | category | flops | bytes accessed | tf_op | source)
XLA Modules:
  0.0 128.8 jit_solution(18092402936943667343)
XLA Ops:
  0.6 125.9 %shard_map.77 = f32[2,128,1024]{2,1,0:T(8,128)} custom-call(s32[4]{0:T(128)} %counts.1, f32[128,4,16,128]{3,2,1,0:T(8,128)} %psi_in.1, f32[4,16,128]{2,1,0:T(8,128)} %pot.1, f32[72,4,16,128]{3,2,1,0:T(8,128)} %bitcast.7, f32[18,4,18]{2,1,0:T(4,128)} %bitcast.8, f32[18,4,18]{2,1,0:T(4,128)} %bitcast.9), custom_call_target="tpu_custom_call" | custom-call | tf_op jit(solution)/shard_map/pallas_call | solution.py:863
  126.6 2.3 %slice_bitcast_fusion = (f32[128,1024]{1,0:T(8,128)}, f32[128,1024]{1,0:T(8,128)}) fusion(f32[2,128,1024]{2,1,0:T(8,128)} %shard_map.77), kind=kLoop, calls=%fused_computation | loop fusion | bytes 2097152 | tf_op jit(solution)/shard_map/squeeze | solution.py:893

commit v6 on v5

--- a/solution.py
+++ b/solution.py
@@ -590,12 +590,16 @@
         @pl.when(t == steps - 3)
         def _():
             with_edges(0)
+            if fused:
+                combine.first_send()
 
         return carry
 
     lax.fori_loop(0, steps - 1, second_phase, 0)
     between = (line > 0) & (line < last)
     take(1, ny - 2)
+    if fused:
+        combine.first_fold()
     partner_row(ny - 1, 0)
 
     @pl.when(between)
@@ -637,6 +641,7 @@
             combine.send(0)
             combine.reduce(0)
         combine.send(1)
+        combine.first_close()
         combine.reduce(1)
         combine.rest()
 
@@ -733,10 +738,13 @@
         def onward(s, group):
             return piece(s, group, 1 - kind, pass_send, pass_recv, other_core)
 
+        def blocks(group):
+            return closing if group else others
+
         def send(group):
             @pl.when(core == 1 - group)
             def _():
-                for s in order:
+                for s in order if group else others:
                     to_core(group, s).start()
 
         def flush(s, group, k):
@@ -744,23 +752,49 @@
             at = (k, slice(None), pl.ds(pl.multiple_of(block * bands, bands), bands))
             pltpu.make_async_copy(result.at[at], out.at[at], out_sem.at[0]).start()
 
+        def fold(group, s):
+            to_core(group, s).wait_recv()
+            both[s] = grid[s, rows(group)] + from_core[s]
+            to_chip(s).start()
+
+        def close(group, s, value):
+            block = s * 2 + (side if group == 0 else 1 - side)
+            result[kind, :, pl.ds(pl.multiple_of(block * bands, bands), bands)] = volume * value
+            far(s, group, kind).start()
+            near(s, group).start()
+            flush(s, group, kind)
+
+        def first_send():
+            @pl.when(core == 1)
+            def _():
+                to_core(0, line).start()
+
+        def first_fold():
+            @pl.when(core == 0)
+            def _():
+                fold(0, line)
+
+        def first_close():
+            @pl.when(core == 0)
+            def _():
+                to_chip(line).wait_recv()
+                close(0, line, both[line, my_kind] + from_chip[line])
+
         def reduce(group):
             @pl.when(core == group)
             def _():
-                for s in order:
-                    to_core(group, s).wait_recv()
-                    both[s] = grid[s, rows(group)] + from_core[s]
-                    to_chip(s).start()
+                for s in order if group else others:
+                    fold(group, s)
 
         def work(group):
-            for s in order:
+            for s in order if group else others:
                 to_chip(s).wait_recv()
                 total[s] = both[s, my_kind] + from_chip[s]
                 if s is not line:
                     to_line(s).start()
                 if group:
                     to_side(s).start()
-            for s in closing:
+            for s in blocks(group):
                 if group:
                     to_side(s).wait_recv()
                     value = swapped[s]
@@ -769,11 +803,7 @@
                 if s is not line:
                     from_line(s).wait_recv()
                     value = value + jnp.transpose(mirror[s])
-                block = s * 2 + (side if group == 0 else 1 - side)
-                result[kind, :, pl.ds(pl.multiple_of(block * bands, bands), bands)] = volume * value
-                far(s, group, kind).start()
-                near(s, group).start()
-                flush(s, group, kind)
+                close(group, s, value)
             for s in closing:
                 near(s, 1 - group).wait_recv()
                 flush(s, 1 - group, kind)
@@ -801,6 +831,7 @@
                     work(group)
 
         self.send = send
+        self.first_send, self.first_fold, self.first_close = first_send, first_fold, first_close
         self.reduce = reduce
         self.rest = rest
 

time: 129 us -> 129 us (level)
  no operation moved by 1% of the time
where the time goes in v6:
time: 129 us
  Pallas kernels  126 us (98%)
  local copies, waits for them, and re-layouts  2.28 us (2%)
    pallas_call x1, Pallas kernels, gram(): pl.pallas_call(functools.partial(gram_kernel, lines, doms, fused, volume)...  126 us

profile of v6, /device:TPU:0, one launch (start us, length us, event | category | flops | bytes accessed | tf_op | source)
XLA Modules:
  0.0 128.9 jit_solution(3438720662022778118)
XLA Ops:
  0.6 125.9 %shard_map.77 = f32[2,128,1024]{2,1,0:T(8,128)} custom-call(s32[4]{0:T(128)} %counts.1, f32[128,4,16,128]{3,2,1,0:T(8,128)} %psi_in.1, f32[4,16,128]{2,1,0:T(8,128)} %pot.1, f32[72,4,16,128]{3,2,1,0:T(8,128)} %bitcast.7, f32[18,4,18]{2,1,0:T(4,128)} %bitcast.8, f32[18,4,18]{2,1,0:T(4,128)} %bitcast.9), custom_call_target="tpu_custom_call" | custom-call | tf_op jit(solution)/shard_map/pallas_call | solution.py:894
  126.6 2.3 %slice_bitcast_fusion = (f32[128,1024]{1,0:T(8,128)}, f32[128,1024]{1,0:T(8,128)}) fusion(f32[2,128,1024]{2,1,0:T(8,128)} %shard_map.77), kind=kLoop, calls=%fused_computation | loop fusion | bytes 2097152 | tf_op jit(solution)/shard_map/squeeze | solution.py:924
